TPU v7x, 32 devices: a whole 2x2x4 slice. The times are simulated.
32 devices in a mesh: pair: 2 (over x), tp: 4 (over z), side: 4 (over y, core).
Axes of the slice: x: 2, y: 2, z: 4, core: 2. Of those that a mesh axis runs over, the one named last changes fastest.
Arguments:
- x_prompt: bfloat16 [2048, 4096], P(('pair', 'side')), parts along dimension 0
- s_len: int32 [8], P(('pair', 'side')), parts along dimension 0
- y_tok: bfloat16 [64, 4096], P(('pair', 'side')), parts along dimension 0
- k_cache: bfloat16 [1, 64, 256, 8, 4, 128], P(None, ('pair', 'side'), None, None, 'tp'), parts along dimension 1
- v_cache: bfloat16 [1, 64, 256, 8, 4, 128], P(None, ('pair', 'side'), None, None, 'tp'), parts along dimension 1
- c_len: int32 [64], P(('pair', 'side')), parts along dimension 0
- wqkv_a: bfloat16 [1, 4096, 32, 384], P(None, None, 'tp')
- wo_a: bfloat16 [1, 32, 128, 4096], P(None, 'tp')
- wug_a: bfloat16 [1, 4096, 2, 11008], P(None, None, None, 'tp')
- wd_a: bfloat16 [1, 11008, 4096], P(None, 'tp')
- norm_a: bfloat16 [1, 2, 4096], replicated
- wqkv_b: bfloat16 [1, 4096, 8, 4, 384], P(None, None, None, 'tp')
- wo_b: bfloat16 [1, 8, 4, 128, 4096], P(None, None, 'tp')
- wug_b: bfloat16 [1, 4096, 2, 11008], P(None, None, None, 'tp')
- wd_b: bfloat16 [1, 11008, 4096], P(None, 'tp')
- norm_b: bfloat16 [1, 2, 4096], replicated
Outputs:
- output 1: bfloat16 [2048, 4096], P(('pair', 'side')), parts along dimension 0
- output 2: bfloat16 [64, 4096], P(('pair', 'side')), parts along dimension 0
- output 3: bfloat16 [1, 2048, 8, 4, 128], P(None, ('pair', 'side'), None, 'tp'), parts along dimension 1
- output 4: bfloat16 [1, 2048, 8, 4, 128], P(None, ('pair', 'side'), None, 'tp'), parts along dimension 1
- output 5: bfloat16 [1, 64, 256, 8, 4, 128], P(None, ('pair', 'side'), None, None, 'tp'), parts along dimension 1
- output 6: bfloat16 [1, 64, 256, 8, 4, 128], P(None, ('pair', 'side'), None, None, 'tp'), parts along dimension 1
There are 2 independent parts. A program takes and returns all parts, laid end to end along the dimension named above; an argument that names none is the same for every part.
All inputs are finite; a program needn't handle non-finite values.
Results may differ from a plain program's by a relative error of at most 0.007746.
Values are sent between devices in bfloat16 or wider.
A program may use at most 1 GiB of HBM per device.

v0:
```python
import jax
import jax.numpy as jnp
from jax import lax
from jax.sharding import PartitionSpec as P

ROPE_BASE = 10000.0
NORM_EPS = 1e-5


def rms_norm(hidden, gain):
    val_f32 = hidden.astype(jnp.float32)
    inv_rms = lax.rsqrt(jnp.mean(val_f32 * val_f32, axis=-1, keepdims=True) + NORM_EPS)
    return (val_f32 * inv_rms * gain.astype(jnp.float32)).astype(jnp.bfloat16)


def rope_rot(vals_in, positions):
    half_dim = vals_in.shape[-1] // 2
    inv_freq = ROPE_BASE ** (-jnp.arange(half_dim, dtype=jnp.float32) / half_dim)
    angles = positions.astype(jnp.float32)[:, None] * inv_freq[None, :]
    tab_shape = (angles.shape[0],) + (1,) * (vals_in.ndim - 2) + (half_dim,)
    cos_tab = jnp.cos(angles).reshape(tab_shape)
    sin_tab = jnp.sin(angles).reshape(tab_shape)
    lo_half = vals_in[..., :half_dim].astype(jnp.float32)
    hi_half = vals_in[..., half_dim:].astype(jnp.float32)
    return jnp.concatenate([lo_half * cos_tab - hi_half * sin_tab, hi_half * cos_tab + lo_half * sin_tab], axis=-1).astype(jnp.bfloat16)


def mlp_block(hidden, w_ug, w_down, gain, combine):
    normed = rms_norm(hidden, gain)
    upgate = jnp.einsum('sd,dkf->skf', normed, w_ug, preferred_element_type=jnp.float32).astype(jnp.bfloat16)
    act_out = (jax.nn.silu(upgate[:, 1].astype(jnp.float32)) * upgate[:, 0].astype(jnp.float32)).astype(jnp.bfloat16)
    mlp_down = combine(jnp.dot(act_out, w_down, preferred_element_type=jnp.float32)).astype(jnp.bfloat16)
    return (hidden.astype(jnp.float32) + mlp_down.astype(jnp.float32)).astype(jnp.bfloat16)


def prompt_layer(hidden, q_start, prev_k, prev_v, seq_len, w_qkv, w_out, w_ug, w_down, gain_pair, combine):
    num_rows = hidden.shape[0]
    kv_loc = w_qkv.shape[1]
    head_dim = (w_qkv.shape[2] - w_out.shape[1]) // 2
    group = w_out.shape[1] // head_dim
    positions = q_start + jnp.arange(num_rows)
    normed = rms_norm(hidden, gain_pair[0])
    qkv_all = jnp.einsum('sd,dhe->she', normed, w_qkv, preferred_element_type=jnp.float32).astype(jnp.bfloat16)
    qkv_all = qkv_all.reshape(num_rows, kv_loc, group + 2, head_dim)
    queries = rope_rot(qkv_all[:, :, :group], positions)
    key_new = rope_rot(qkv_all[:, :, group], positions)
    val_new = qkv_all[:, :, group + 1]
    if prev_k is None:
        key_all = key_new
        val_all = val_new
    else:
        key_all = jnp.concatenate([prev_k, key_new], axis=0)
        val_all = jnp.concatenate([prev_v, val_new], axis=0)
    key_pos = jnp.arange(key_all.shape[0])
    allowed = (key_pos[None, :] <= positions[:, None]) & (key_pos[None, :] < seq_len)
    scores = jnp.einsum('qhgd,khd->hgqk', queries, key_all, preferred_element_type=jnp.float32) * head_dim ** -0.5
    scores = jnp.where(allowed, scores, -1e30)
    attn_prob = jax.nn.softmax(scores, axis=-1).astype(jnp.bfloat16)
    attn_out = jnp.einsum('hgqk,khd->qhgd', attn_prob, val_all, preferred_element_type=jnp.float32).astype(jnp.bfloat16)
    attn_proj = combine(jnp.einsum('qhf,hfd->qd', attn_out.reshape(num_rows, kv_loc, group * head_dim), w_out, preferred_element_type=jnp.float32)).astype(jnp.bfloat16)
    hidden = (hidden.astype(jnp.float32) + attn_proj.astype(jnp.float32)).astype(jnp.bfloat16)
    hidden = mlp_block(hidden, w_ug, w_down, gain_pair[1], combine)
    return hidden, key_new, val_new


def prefill_side(x_rows, seq_len, wqkv, wo, wug, wd, norms, combine):
    num_layers = wqkv.shape[0]
    half_len = x_rows.shape[0] // 2
    hidden_first = x_rows[:half_len]
    first_keys = []
    first_vals = []
    for layer_idx in range(num_layers):
        hidden_first, key_new, val_new = prompt_layer(hidden_first, 0, None, None, seq_len, wqkv[layer_idx], wo[layer_idx], wug[layer_idx], wd[layer_idx], norms[layer_idx], combine)
        first_keys.append(key_new)
        first_vals.append(val_new)
    hidden_second = x_rows[half_len:]
    key_layers = []
    val_layers = []
    for layer_idx in range(num_layers):
        hidden_second, key_new, val_new = prompt_layer(hidden_second, half_len, first_keys[layer_idx], first_vals[layer_idx], seq_len, wqkv[layer_idx], wo[layer_idx], wug[layer_idx], wd[layer_idx], norms[layer_idx], combine)
        key_layers.append(jnp.concatenate([first_keys[layer_idx], key_new], axis=0))
        val_layers.append(jnp.concatenate([first_vals[layer_idx], val_new], axis=0))
    valid = (jnp.arange(x_rows.shape[0]) < seq_len)[None, :, None, None]
    zero_val = jnp.zeros((), jnp.bfloat16)
    key_cache = jnp.where(valid, jnp.stack(key_layers), zero_val)
    val_cache = jnp.where(valid, jnp.stack(val_layers), zero_val)
    return jnp.concatenate([hidden_first, hidden_second], axis=0), key_cache, val_cache


def decode_side(tokens, lengths, k_cache, v_cache, wqkv, wo, wug, wd, norms, combine):
    num_layers = wqkv.shape[0]
    batch_rows = tokens.shape[0]
    kv_loc = wqkv.shape[2]
    tp_loc = wqkv.shape[3]
    head_dim = (wqkv.shape[4] - wo.shape[3]) // 2
    group = wo.shape[3] // head_dim
    slot_pos = jnp.arange(k_cache.shape[2])
    write_slot = (slot_pos[None, :] == lengths[:, None])[:, :, None, None, None]
    visible = (slot_pos[None, :] <= lengths[:, None])[:, None, None, None, :]
    hidden = tokens
    new_keys = []
    new_vals = []
    for layer_idx in range(num_layers):
        normed = rms_norm(hidden, norms[layer_idx, 0])
        qkv_all = jnp.einsum('bd,dije->bije', normed, wqkv[layer_idx], preferred_element_type=jnp.float32).astype(jnp.bfloat16)
        qkv_all = qkv_all.reshape(batch_rows, kv_loc, tp_loc, group + 2, head_dim)
        queries = rope_rot(qkv_all[:, :, :, :group], lengths)
        key_new = rope_rot(qkv_all[:, :, :, group], lengths)
        val_new = qkv_all[:, :, :, group + 1]
        key_upd = jnp.where(write_slot, key_new[:, None], k_cache[layer_idx])
        val_upd = jnp.where(write_slot, val_new[:, None], v_cache[layer_idx])
        scores = jnp.einsum('bijge,bsije->bijgs', queries, key_upd, preferred_element_type=jnp.float32) * head_dim ** -0.5
        scores = jnp.where(visible, scores, -1e30)
        attn_prob = jax.nn.softmax(scores, axis=-1).astype(jnp.bfloat16)
        attn_out = jnp.einsum('bijgs,bsije->bijge', attn_prob, val_upd, preferred_element_type=jnp.float32).astype(jnp.bfloat16)
        attn_proj = combine(jnp.einsum('bijf,ijfd->bd', attn_out.reshape(batch_rows, kv_loc, tp_loc, group * head_dim), wo[layer_idx], preferred_element_type=jnp.float32)).astype(jnp.bfloat16)
        hidden = (hidden.astype(jnp.float32) + attn_proj.astype(jnp.float32)).astype(jnp.bfloat16)
        hidden = mlp_block(hidden, wug[layer_idx], wd[layer_idx], norms[layer_idx, 1], combine)
        new_keys.append(key_upd)
        new_vals.append(val_upd)
    return hidden, jnp.stack(new_keys), jnp.stack(new_vals)


def tp_relayout(block, tp_size):
    num_layers, seq_rows, kv_loc, head_dim = block.shape
    if kv_loc % tp_size == 0:
        split_view = block.reshape(num_layers, seq_rows, kv_loc // tp_size, tp_size, head_dim)
        return lax.all_to_all(split_view, 'tp', 3, 2, tiled=True)
    ratio = tp_size // kv_loc
    tp_idx = lax.axis_index('tp')
    src_block = tp_idx // ratio
    dst_pos = tp_idx % kv_loc
    gathered = jnp.zeros_like(block)
    for round_idx in range(kv_loc):
        piece = lax.dynamic_slice_in_dim(block, (round_idx + src_block) % kv_loc, 1, axis=2)
        perm_pairs = [(src, (src % ratio) * kv_loc + (round_idx + src // ratio) % kv_loc) for src in range(tp_size)]
        received = lax.ppermute(piece, 'tp', perm_pairs)
        gathered = lax.dynamic_update_slice_in_dim(gathered, received, (dst_pos - round_idx) % kv_loc, axis=2)
    return gathered[:, :, :, None]


def hand_off(block, tp_size, side_size):
    shift_pairs = [(src, (src + side_size // 2) % side_size) for src in range(side_size)]
    moved = lax.ppermute(block, 'side', shift_pairs)
    return tp_relayout(moved, tp_size)


def solution(mesh):
    tp_size = mesh.shape['tp']
    side_size = mesh.shape['side']
    rows_spec = P(('pair', 'side'), None)
    flat_spec = P(('pair', 'side'))
    cache_spec = P(None, ('pair', 'side'), None, None, 'tp', None)
    prompt_spec = P(None, ('pair', 'side'), None, 'tp', None)
    in_specs = (rows_spec, flat_spec, rows_spec, cache_spec, cache_spec, flat_spec,
                P(None, None, 'tp', None), P(None, 'tp', None, None), P(None, None, None, 'tp'), P(None, 'tp', None), P(),
                P(None, None, None, 'tp', None), P(None, None, 'tp', None, None), P(None, None, None, 'tp'), P(None, 'tp', None), P())
    out_specs = (rows_spec, rows_spec, prompt_spec, prompt_spec, cache_spec, cache_spec)

    def tp_sum(part_sum):
        return lax.psum(part_sum, 'tp')

    def body(x_prompt, s_len, y_tok, k_cache, v_cache, c_len, wqkv_a, wo_a, wug_a, wd_a, norm_a, wqkv_b, wo_b, wug_b, wd_b, norm_b):
        hidden, key_cache, val_cache = prefill_side(x_prompt, s_len[0], wqkv_a, wo_a, wug_a, wd_a, norm_a, tp_sum)
        k_prompt = hand_off(key_cache, tp_size, side_size)
        v_prompt = hand_off(val_cache, tp_size, side_size)
        y_out, k_new, v_new = decode_side(y_tok, c_len, k_cache, v_cache, wqkv_b, wo_b, wug_b, wd_b, norm_b, tp_sum)
        return hidden, y_out, k_prompt, v_prompt, k_new, v_new

    return jax.shard_map(body, mesh=mesh, in_specs=in_specs, out_specs=out_specs, check_vma=False)
```

profile of v0, /device:TPU:0, one launch (start us, length us, event | category | flops | bytes accessed | tf_op | source)
XLA Modules:
  0.0 523.1 jit_solution(1467098627624964366)
XLA Ops:
  1.7 2.0 fusion.48
  4.6 15.7 %fusion.77 = bf16[128,8,384]{2,0,1:T(8,128)(2,1)} fusion(bf16[4096,8,384]{2,1,0:T(8,128)(2,1)} %bitcast.241, f32[128]{0:T(128)S(1)} %get-tuple-element.82, f32[4096]{0:T(1024)S(1)} %bitcast.239, bf16[256,4096]{1,0:T(8,128)(2,1)S(1)} %copy-done.1), kind=kOutput, calls=%fused_computation.84 | convolution fusion | flops 3223715840 | bytes 27017728 | tf_op jit(solution)/shard_map/sd,dhe->she/dot_general | solution.py:43
  22.7 16.2 %fusion.74 = bf16[128,8,384]{2,0,1:T(8,128)(2,1)} fusion(bf16[4096,8,384]{2,1,0:T(8,128)(2,1)} %bitcast.242, f32[4096]{0:T(1024)S(1)} %bitcast.240, f32[128]{0:T(128)S(1)} %get-tuple-element.83, bf16[256,4096]{1,0:T(8,128)(2,1)S(1)} %copy-done.1), kind=kOutput, calls=%fused_computation.83 | convolution fusion | flops 3223715840 | bytes 27017728 | tf_op jit(solution)/shard_map/sd,dhe->she/dot_general | solution.py:43
  44.3 3.0 collective-permute-start
  50.0 13.5 %fusion.92 = bf16[8,8,1,3,128]{4,0,3,1,2:T(8,128)(2,1)S(1)} fusion(bf16[4096,8,384]{2,1,0:T(8,128)(2,1)} %bitcast.222, bf16[8,4096]{1,0:T(8,128)(2,1)S(1)} %copy-done.9, f32[4096]{0:T(1024)S(1)} %bitcast.238, f32[8]{0:T(128)S(1)} %add_rsqrt_fusion.1), kind=kOutput, calls=%fused_computation.99 | convolution fusion | flops 201482240 | bytes 25296928 | tf_op jit(solution)/shard_map/bd,dije->bije/dot_general | solution.py:105
  67.2 5.0 fusion.29
  75.2 6.2 %fusion.26 = f32[128,4096]{1,0:T(8,128)} fusion(bf16[1,8,128,4096]{3,2,1,0:T(8,128)(2,1)} %param.23, f32[8,1,128,128]{2,3,0,1:T(8,128)S(1)} %get-tuple-element.81, f32[8,128]{1,0:T(8,128)S(1)} %fusion.153, f32[8,128]{1,0:T(8,128)S(1)} %get-tuple-element.80, bf16[128,8,1,128]{3,1,2,0:T(8,128)(2,1)S(1)} %copy-done.6), kind=kOutput, calls=%fused_computation.26 | convolution fusion | flops 1107820544 | bytes 11280384 | tf_op jit(solution)/shard_map/qhf,hfd->qd/dot_general | solution.py:60
  81.7 8.5 %bitcast_select_fusion.1 = (bf16[8,256,8,128]{3,2,1,0:T(8,128)(2,1)S(1)}, bf16[8,256,8,128]{3,2,1,0:T(8,128)(2,1)}) fusion(bf16[1,8,256,8,1,128]{5,3,4,2,1,0:T(8,128)(2,1)} %param.19, pred[8,256]{1,0:T(8,128)(4,1)S(1)} %copy-done.21, bf16[8,8,128]{2,1,0:T(8,128)(2,1)S(1)} %copy.128, bf16[1,8,256,8,1,128]{5,3,4,2,1,0:T(8,128)(2,1)} %param.20, ...), kind=kLoop, calls=%fused_computation.30 | loop fusion | flops 4194304 | bytes 16812032 | tf_op jit(solution)/shard_map/jit(_where)/select_n | solution.py:110
  91.6 2.8 fusion.35
  94.5 4.6 fusion.32
  99.1 151.6 %all-reduce.4 = (bf16[128,4096]{1,0:T(8,128)(2,1)S(1)}, bf16[128,4096]{1,0:T(8,128)(2,1)}, bf16[8,4096]{1,0:T(8,128)(2,1)S(1)}) all-reduce(f32[128,4096]{1,0:T(8,128)S(1)} %fusion.29, f32[128,4096]{1,0:T(8,128)} %fusion.26, f32[8,4096]{1,0:T(8,128)S(1)} %fusion.32), channel_id=1, replica_groups=mesh['pair'=2,'tp'=4,'side'=4] {'tp'}, use_global_device_ids=true, to_apply=%region_9.10 | all-reduce | flops 1081344 | bytes 6488064 | tf_op jit(solution)/shard_map/psum | solution.py:161
  250.7 2.8 fusion.52
  253.5 18.4 %fusion.42 = bf16[128,2,2752]{0,2,1:T(8,128)(2,1)S(1)} fusion(bf16[1,4096,2,2752]{1,3,2,0:T(8,128)(2,1)} %param.24, bf16[128,4096]{1,0:T(8,128)(2,1)S(1)} %get-tuple-element.33, f32[128]{0:T(128)S(1)} %add_rsqrt_fusion.2, f32[4096]{0:T(1024)S(1)} %bitcast.235), kind=kOutput, calls=%fused_computation.38 | convolution fusion | flops 5774163968 | bytes 47563264 | tf_op jit(solution)/shard_map/sd,dkf->skf/dot_general | solution.py:30
  271.9 12.0 %fusion.12 = f32[128,4096]{1,0:T(8,128)} fusion(bf16[1,2752,4096]{2,1,0:T(8,128)(2,1)} %param.25, bf16[128,2,2752]{0,2,1:T(8,128)(2,1)S(1)} %fusion.42), kind=kOutput, calls=%fused_computation.12 | convolution fusion | flops 2888499200 | bytes 26050560 | tf_op jit(solution)/shard_map/dot_general | solution.py:32
  283.9 18.6 %fusion.39 = bf16[128,2,2752]{0,2,1:T(8,128)(2,1)S(1)} fusion(bf16[1,4096,2,2752]{1,3,2,0:T(8,128)(2,1)} %param.24, bf16[128,4096]{1,0:T(8,128)(2,1)S(1)} %get-tuple-element.29, f32[4096]{0:T(1024)S(1)} %bitcast.236, f32[128]{0:T(128)S(1)} %add_rsqrt_fusion.4), kind=kOutput, calls=%fused_computation.37 | convolution fusion | flops 5774163968 | bytes 47563264 | tf_op jit(solution)/shard_map/sd,dkf->skf/dot_general | solution.py:30
  302.5 12.0 %fusion.14 = f32[128,4096]{1,0:T(8,128)} fusion(bf16[1,2752,4096]{2,1,0:T(8,128)(2,1)} %param.25, bf16[128,2,2752]{0,2,1:T(8,128)(2,1)S(1)} %fusion.39), kind=kOutput, calls=%fused_computation.14 | convolution fusion | flops 2888499200 | bytes 26050560 | tf_op jit(solution)/shard_map/dot_general | solution.py:32
  314.7 18.7 %fusion.45 = bf16[8,2,2752]{2,0,1:T(8,128)(2,1)S(1)} fusion(bf16[1,4096,2,2752]{1,3,2,0:T(8,128)(2,1)} %param.29, bf16[8,4096]{1,0:T(8,128)(2,1)S(1)} %get-tuple-element.27, f32[4096]{0:T(1024)S(1)} %bitcast.237, f32[8]{0:T(128)S(1)} %add_rsqrt_fusion), kind=kOutput, calls=%fused_computation.39 | convolution fusion | flops 360885248 | bytes 45258784 | tf_op jit(solution)/shard_map/sd,dkf->skf/dot_general | solution.py:30
  333.4 9.0 %fusion.10 = f32[8,4096]{1,0:T(8,128)S(1)} fusion(bf16[1,2752,4096]{2,1,0:T(8,128)(2,1)} %param.30, bf16[8,2,2752]{2,0,1:T(8,128)(2,1)S(1)} %fusion.45), kind=kOutput, calls=%fused_computation.10 | convolution fusion | flops 180531200 | bytes 22763520 | tf_op jit(solution)/shard_map/dot_general | solution.py:32
  342.4 145.3 %all-reduce.5 = (bf16[128,4096]{1,0:T(8,128)(2,1)}, bf16[128,4096]{1,0:T(8,128)(2,1)}, bf16[8,4096]{1,0:T(8,128)(2,1)S(1)}) all-reduce(f32[128,4096]{1,0:T(8,128)} %fusion.12, f32[128,4096]{1,0:T(8,128)} %fusion.14, f32[8,4096]{1,0:T(8,128)S(1)} %fusion.10), channel_id=1, replica_groups=mesh['pair'=2,'tp'=4,'side'=4] {'tp'}, use_global_device_ids=true, to_apply=%region_11.12 | all-reduce | flops 1081344 | bytes 6488064 | tf_op jit(solution)/shard_map/psum | solution.py:161
  489.6 1.9 copy.130
  491.5 4.1 all-to-all-start
  498.1 7.6 %all-to-all-done = bf16[1,256,2,4,128]{4,1,2,0,3:T(8,128)(2,1)S(1)} async-done(((bf16[1,256,2,4,128]{4,1,2,0,3:T(8,128)(2,1)}), bf16[1,256,2,4,128]{4,1,2,0,3:T(8,128)(2,1)S(1)}, u32[]{:S(2)}, u32[]{:S(2)}) %all-to-all-start) | async-done | bytes 524320 | tf_op jit(solution)/shard_map/all_to_all | solution.py:128
  505.6 3.5 all-to-all-start.1
  512.1 8.3 %broadcast_select_fusion = (bf16[1,8,256,8,1,128]{5,3,4,2,1,0:T(8,128)(2,1)}, bf16[1,8,256,8,1,128]{5,3,4,2,1,0:T(8,128)(2,1)}) fusion(bf16[1,8,256,8,1,128]{5,3,4,2,1,0:T(8,128)(2,1)} %param.20, pred[8,256]{1,0:T(8,128)(4,1)S(1)} %copy-done.21, bf16[8,8,128]{2,1,0:T(8,128)(2,1)S(1)} %copy.129, bf16[1,8,256,8,1,128]{5,3,4,2,1,0:T(8,128)(2,1)S(1)} %copy-done, ...), kind=kLoop, calls=%fused_computation.35 | loop fusion | flops 4194304 | bytes 16812032 | tf_op jit(solution)/shard_map/jit(_where)/select_n | solution.py:111
  (118 shorter events, 29.3 us)
Async XLA Ops:
  0.6 3.9 copy-start.1
  38.9 2.6 copy-start.23
  38.9 2.6 copy-start.25
  42.7 23.1 %copy-start.3 = (bf16[128,8,64]{2,0,1:T(8,128)(2,1)}, bf16[128,8,64]{2,0,1:T(8,128)(2,1)S(1)}, u32[]{:S(2)}) copy-start(bf16[128,8,64]{2,0,1:T(8,128)(2,1)S(1)} %get-tuple-element.46) | copy-start | bytes 393220
  42.7 23.1 %copy-start.4 = (bf16[128,8,64]{2,0,1:T(8,128)(2,1)}, bf16[128,8,64]{2,0,1:T(8,128)(2,1)S(1)}, u32[]{:S(2)}) copy-start(bf16[128,8,64]{2,0,1:T(8,128)(2,1)S(1)} %get-tuple-element.47) | copy-start | bytes 393220
  42.9 5.5 %copy-start.27 = (s32[8]{0:T(128)S(1)}, s32[8]{0:T(128)}, u32[]{:S(2)}) copy-start(s32[8]{0:T(128)} %param.21) | copy-start | bytes 100
  42.9 6.3 %copy-start.19 = (bf16[1,2,4096]{2,1,0:T(2,128)(2,1)S(1)}, bf16[1,2,4096]{2,1,0:T(2,128)(2,1)}, u32[]{:S(2)}) copy-start(bf16[1,2,4096]{2,1,0:T(2,128)(2,1)} %param.31) | copy-start | bytes 49156
  42.9 6.9 %copy-start.9 = (bf16[8,4096]{1,0:T(8,128)(2,1)S(1)}, bf16[8,4096]{1,0:T(8,128)(2,1)}, u32[]{:S(2)}) copy-start(bf16[8,4096]{1,0:T(8,128)(2,1)} %param.18) | copy-start | bytes 196612
  44.3 445.3 %collective-permute-start = (bf16[1,256,8,128]{3,1,2,0:T(8,128)(2,1)}, bf16[1,256,8,128]{3,1,2,0:T(8,128)(2,1)}, u32[]{:S(2)}, u32[]{:S(2)}) collective-permute-start(bf16[1,256,8,128]{3,1,2,0:T(8,128)(2,1)} %get-tuple-element.73), channel_id=1, source_target_pairs={{0,2},{1,3},{2,0},{3,1},{4,6},{5,7},{6,4},{7,5},{8,10},{9,11},{10,... | collective-permute-start | bytes 1572872 | tf_op jit(solution)/shard_map/ppermute | solution.py:144
  47.3 448.9 %collective-permute-start.1 = (bf16[1,256,8,128]{3,1,2,0:T(8,128)(2,1)}, bf16[1,256,8,128]{3,1,2,0:T(8,128)(2,1)}, u32[]{:S(2)}, u32[]{:S(2)}) collective-permute-start(bf16[1,256,8,128]{3,1,2,0:T(8,128)(2,1)} %get-tuple-element.72), channel_id=1, source_target_pairs={{0,2},{1,3},{2,0},{3,1},{4,6},{5,7},{6,4},{7,5},{8,10},{9,11},{10,... | collective-permute-start | bytes 1572872 | tf_op jit(solution)/shard_map/ppermute | solution.py:144
  49.2 15.7 %copy-start.13 = (f32[8,64]{1,0:T(8,128)}, f32[8,64]{1,0:T(8,128)S(1)}, u32[]{:S(2)}) copy-start(f32[8,64]{1,0:T(8,128)S(1)} %get-tuple-element.66) | copy-start | bytes 6148
  49.2 15.7 %copy-start.15 = (f32[8,64]{1,0:T(8,128)}, f32[8,64]{1,0:T(8,128)S(1)}, u32[]{:S(2)}) copy-start(f32[8,64]{1,0:T(8,128)S(1)} %get-tuple-element.67) | copy-start | bytes 6148
  72.2 2.9 copy-start.6
  75.2 6.3 %copy-start.11 = (bf16[8,8,1,128]{3,0,1,2:T(8,128)(2,1)S(1)}, bf16[8,8,1,128]{3,0,1,2:T(8,128)(2,1)}, u32[]{:S(2)}) copy-start(bf16[8,8,1,128]{3,0,1,2:T(8,128)(2,1)} %get-tuple-element.54) | copy-start | bytes 49156
  75.2 6.3 %copy-start.14 = (f32[8,64]{1,0:T(8,128)S(1)}, f32[8,64]{1,0:T(8,128)}, u32[]{:S(2)}) copy-start(f32[8,64]{1,0:T(8,128)} %copy-done.13) | copy-start | bytes 6148
  75.2 6.3 %copy-start.16 = (f32[8,64]{1,0:T(8,128)S(1)}, f32[8,64]{1,0:T(8,128)}, u32[]{:S(2)}) copy-start(f32[8,64]{1,0:T(8,128)} %copy-done.15) | copy-start | bytes 6148
  75.2 6.4 %copy-start.20 = (bf16[8,8,128]{2,0,1:T(8,128)(2,1)S(1)}, bf16[8,8,128]{2,0,1:T(8,128)(2,1)}, u32[]{:S(2)}) copy-start(bf16[8,8,128]{2,0,1:T(8,128)(2,1)} %get-tuple-element.55) | copy-start | bytes 49156
  75.2 6.4 %copy-start.17 = (bf16[8,8,64]{2,0,1:T(8,128)(2,1)S(1)}, bf16[8,8,64]{2,0,1:T(8,128)(2,1)}, u32[]{:S(2)}) copy-start(bf16[8,8,64]{2,0,1:T(8,128)(2,1)} %fusion.214) | copy-start | bytes 24580
  75.2 6.4 %copy-start.18 = (bf16[8,8,64]{2,0,1:T(8,128)(2,1)S(1)}, bf16[8,8,64]{2,0,1:T(8,128)(2,1)}, u32[]{:S(2)}) copy-start(bf16[8,8,64]{2,0,1:T(8,128)(2,1)} %fusion.215) | copy-start | bytes 24580
  75.2 6.5 %copy-start.21 = (pred[8,256]{1,0:T(8,128)(4,1)S(1)}, pred[8,256]{1,0:T(8,128)(4,1)}, u32[]{:S(2)}) copy-start(pred[8,256]{1,0:T(8,128)(4,1)} %get-tuple-element.75) | copy-start | bytes 6148
  302.5 12.1 %copy-start.12 = (f32[1,1,4096]{2,1,0:T(1,128)S(1)}, f32[1,1,4096]{2,1,0:T(1,128)}, u32[]{:S(2)}) copy-start(f32[1,1,4096]{2,1,0:T(1,128)} %get-tuple-element.58) | copy-start | bytes 49156
  491.5 14.2 %all-to-all-start = ((bf16[1,256,2,4,128]{4,1,2,0,3:T(8,128)(2,1)}), bf16[1,256,2,4,128]{4,1,2,0,3:T(8,128)(2,1)S(1)}, u32[]{:S(2)}, u32[]{:S(2)}) async-start(bf16[1,256,2,4,128]{4,1,2,0,3:T(8,128)(2,1)} %copy.130), calls=%async_computation | async-start | bytes 1048576 | tf_op jit(solution)/shard_map/all_to_all | solution.py:128
  505.6 15.9 %all-to-all-start.1 = ((bf16[1,256,2,4,128]{4,1,2,0,3:T(8,128)(2,1)}), bf16[1,256,2,4,128]{4,1,2,0,3:T(8,128)(2,1)S(1)}, u32[]{:S(2)}, u32[]{:S(2)}) async-start(bf16[1,256,2,4,128]{4,1,2,0,3:T(8,128)(2,1)} %copy.131), calls=%async_computation.1 | async-start | bytes 1048576 | tf_op jit(solution)/shard_map/all_to_all | solution.py:128
  509.1 2.9 copy-start
  (8 other events, 13.1 us)
where the time goes:
time: 532 us; the launch traced here: 523 us
  blocking collectives  297 us (56%)
  matrix products  156 us (29%)
  other arithmetic  36.1 us (7%)
  local copies, waits for them, and re-layouts  13.4 us (3%)
  starting transfers between devices  10.6 us (2%)
  waiting for transfers between devices  7.57 us (1%)
    psum x2, blocking collectives, tp_sum(): return lax.psum(part_sum, 'tp')  297 us
    dot_general x3, matrix products, mlp_block(): jnp.einsum('sd,dkf->skf', normed, w_ug, preferred_element_type=jnp.float32)  55.8 us
    dot_general x3, matrix products, mlp_block(): jnp.dot(act_out, w_down, preferred_element_type=jnp.float32)  32.9 us
    dot_general x2, matrix products, prompt_layer(): jnp.einsum('sd,dhe->she', normed, w_qkv, preferred_element_type=jnp.float32)  31.9 us
    dot_general x1, matrix products, decode_side(): jnp.einsum('bd,dije->bije', normed, wqkv[layer_idx], preferred_element_ty...  13.5 us
    dot_general x2, matrix products, prompt_layer(): jnp.einsum('qhf,hfd->qd', attn_out.reshape(num_rows, kv_loc, group * head...  11.2 us
  transfers between devices with their start and end apart: 4, of which 1 were waited for; matrix products, arithmetic and copies ran while one was open for 31% of the time, Pallas kernels for 0%

commit v1 on v0

v1 whole, which is shorter than its diff:
```python
import jax
import jax.numpy as jnp
from jax import lax
from jax.experimental import pallas as pl
from jax.experimental.pallas import tpu as pltpu
from jax.sharding import PartitionSpec as P

ROPE_BASE = 10000.0
NORM_EPS = 1e-5


def rms_norm(hidden, gain):
    val_f32 = hidden.astype(jnp.float32)
    inv_rms = lax.rsqrt(jnp.mean(val_f32 * val_f32, axis=-1, keepdims=True) + NORM_EPS)
    return (val_f32 * inv_rms * gain.astype(jnp.float32)).astype(jnp.bfloat16)


def rope_rot(vals_in, positions):
    half_dim = vals_in.shape[-1] // 2
    inv_freq = ROPE_BASE ** (-jnp.arange(half_dim, dtype=jnp.float32) / half_dim)
    angles = positions.astype(jnp.float32)[:, None] * inv_freq[None, :]
    tab_shape = (angles.shape[0],) + (1,) * (vals_in.ndim - 2) + (half_dim,)
    cos_tab = jnp.cos(angles).reshape(tab_shape)
    sin_tab = jnp.sin(angles).reshape(tab_shape)
    lo_half = vals_in[..., :half_dim].astype(jnp.float32)
    hi_half = vals_in[..., half_dim:].astype(jnp.float32)
    return jnp.concatenate([lo_half * cos_tab - hi_half * sin_tab, hi_half * cos_tab + lo_half * sin_tab], axis=-1).astype(jnp.bfloat16)


MESH_ID = pl.DeviceIdType.MESH
COLS = 256
HALF_ROWS = 128
RING = 3
WIRE = 128
SKEW = 2


def block_kernel(x_ref, y_ref, attn_a_ref, attn_b_ref, norm_a_ref, norm_b_ref, wo_a, wug_a, wd_a, wo_b, wug_b, wd_b,
                 out_a, out_b,
                 part, rcv, hid, part_d, rcv_d, hid_d, normed, act, normed_d, act_d, ug_buf, dn_buf,
                 rs_send, rs_recv, ag_send, ag_recv, rsd_send, rsd_recv, agd_send, agd_recv, ug_sem, dn_sem, out_sem):
    ffn, width = wd_a.shape
    mid = width // 2
    per = mid // WIRE
    n_up = -(-ffn // COLS)
    last_up = ffn - COLS
    n_dn = width // 512
    z = lax.axis_index('tp')

    def pos(half):
        return half * z + (1 - half) * (3 - z)

    def fwd(half):
        return lax.rem(z + 4 + (2 * half - 1), 4)

    def bwd(half):
        return lax.rem(z + 4 - (2 * half - 1), 4)

    def remote(src, dst, ssem, rsem, target):
        return pltpu.make_async_remote_copy(src_ref=src, dst_ref=dst, send_sem=ssem, recv_sem=rsem,
                                            device_id={'tp': target}, device_id_type=MESH_ID)

    def rs_copy(half, g):
        return remote(part.at[half, g], rcv.at[half, g], rs_send.at[half], rs_recv.at[half, g], fwd(half))

    def ag_copy(half, g):
        return remote(hid.at[half, g], hid.at[half, g], ag_send.at[half], ag_recv.at[half, g], bwd(half))

    def rsd_copy(ar, half):
        return remote(part_d.at[ar, half], rcv_d.at[ar, half], rsd_send.at[ar, half], rsd_recv.at[ar, half], fwd(half))

    def agd_copy(ar, half):
        return remote(hid_d.at[ar, half], hid_d.at[ar, half], agd_send.at[ar, half], agd_recv.at[ar, half], bwd(half))

    def out_copy(half, g):
        row = (g // per - 2) * HALF_ROWS
        col = pl.multiple_of(half * mid + lax.rem(g, per) * WIRE, WIRE)
        return pltpu.make_async_copy(hid.at[half, g], out_a.at[pl.ds(pl.multiple_of(row, HALF_ROWS), HALF_ROWS), pl.ds(col, WIRE)], out_sem.at[half])

    def ug_copy(src, i, slot):
        row = pl.multiple_of(jnp.minimum(i * COLS, last_up), 64)
        return pltpu.make_async_copy(src.at[:, pl.ds(row, COLS), :], ug_buf.at[slot], ug_sem.at[slot])

    def dn_copy(src, j, slot):
        col = pl.multiple_of(lax.rem(j, 2) * mid + (j // 2) * 512, 512)
        return pltpu.make_async_copy(src.at[:, pl.ds(col, 512)], dn_buf.at[slot, pl.ds(0, src.shape[0]), :], dn_sem.at[slot])

    def slot_step(s, first, last, second, dec_at):
        ar = 1 if second else 0
        for half in range(2):
            where_at = pos(half)
            g = first + s - SKEW * where_at
            back = first + s - SKEW * (6 - where_at)
            dec = s - dec_at

            @pl.when((where_at == 0) & (g < last))
            def _():
                rs_copy(half, g).start()

            @pl.when((where_at > 0) & (where_at < 3) & (g >= first) & (g < last))
            def _():
                rs_copy(half, g).wait_recv()
                part[half, g] = part[half, g] + rcv[half, g]
                rs_copy(half, g).start()

            @pl.when((where_at == 3) & (g >= first) & (g < last))
            def _():
                rs_copy(half, g).wait_recv()
                total = (part[half, g] + rcv[half, g]).astype(jnp.bfloat16).astype(jnp.float32)
                if second:
                    base = hid[half, g - 2 * per]
                else:
                    row = pl.multiple_of((g // per) * HALF_ROWS, HALF_ROWS)
                    col = pl.multiple_of(half * mid + lax.rem(g, per) * WIRE, WIRE)
                    base = x_ref[pl.ds(row, HALF_ROWS), pl.ds(col, WIRE)]
                hid[half, g] = (base.astype(jnp.float32) + total).astype(jnp.bfloat16)
                ag_copy(half, g).start()
                if second:
                    out_copy(half, g).start()

            @pl.when((where_at < 3) & (back >= first) & (back < last))
            def _():
                ag_copy(half, back).wait_recv()

                @pl.when(where_at > 0)
                def _():
                    ag_copy(half, back).start()
                if second:
                    out_copy(half, back).start()

            @pl.when((where_at == 0) & (dec == 0))
            def _():
                rsd_copy(ar, half).start()

            @pl.when((where_at > 0) & (where_at < 3) & (dec == SKEW * where_at))
            def _():
                rsd_copy(ar, half).wait_recv()
                part_d[ar, half] = part_d[ar, half] + rcv_d[ar, half]
                rsd_copy(ar, half).start()

            @pl.when((where_at == 3) & (dec == SKEW * where_at))
            def _():
                rsd_copy(ar, half).wait_recv()
                total = (part_d[ar, half] + rcv_d[ar, half]).astype(jnp.bfloat16).astype(jnp.float32)
                base = hid_d[0, half] if ar else y_ref[:, half * mid:(half + 1) * mid]
                hid_d[ar, half] = (base.astype(jnp.float32) + total).astype(jnp.bfloat16)
                agd_copy(ar, half).start()

            @pl.when((where_at < 3) & (dec == SKEW * (6 - where_at)))
            def _():
                agd_copy(ar, half).wait_recv()

                @pl.when(where_at > 0)
                def _():
                    agd_copy(ar, half).start()

    def up_phase(src, nxt, base, lhs_ref, act_ref, comm):
        def step(i, carry):
            slot = lax.rem(base + i, RING)
            ug_copy(src, i, slot).wait()
            lhs = lhs_ref[...]
            dims = (((1,), (1,)), ((), ()))
            up = lax.dot_general(lhs, ug_buf[slot, 0], dims, preferred_element_type=jnp.float32).astype(jnp.bfloat16).astype(jnp.float32)
            gate = lax.dot_general(lhs, ug_buf[slot, 1], dims, preferred_element_type=jnp.float32).astype(jnp.bfloat16).astype(jnp.float32)
            val = jax.nn.silu(gate) * up
            col = lax.broadcasted_iota(jnp.int32, val.shape, 1) + jnp.minimum(i * COLS, last_up)
            act_ref[i] = jnp.where(col >= i * COLS, val, 0.0).astype(jnp.bfloat16)

            @pl.when(i + RING < n_up)
            def _():
                ug_copy(src, i + RING, slot).start()
            if nxt is not None:
                @pl.when(i + RING >= n_up)
                def _():
                    ug_copy(nxt, i + RING - n_up, slot).start()
            comm(i)
            return carry
        lax.fori_loop(0, n_up, step, 0)

    def dn_phase(src, nxt, base, compute, comm):
        def step(j, carry):
            slot = lax.rem(base + j, RING)
            dn_copy(src, j, slot).wait()
            compute(j, slot)

            @pl.when(j + RING < n_dn)
            def _():
                dn_copy(src, j + RING, slot).start()
            if nxt is not None:
                @pl.when(j + RING >= n_dn)
                def _():
                    dn_copy(nxt, j + RING - n_dn, slot).start()
            comm(j)
            return carry
        lax.fori_loop(0, n_dn, step, 0)

    def down_dot(act_ref, slot):
        total = None
        for i in range(n_up):
            start = min(i * COLS, last_up)
            piece = jnp.dot(act_ref[i], dn_buf[slot, start:start + COLS, :], preferred_element_type=jnp.float32)
            total = piece if total is None else total + piece
        return total

    def put_part(j, first, total):
        half = lax.rem(j, 2)
        for q in range(512 // WIRE):
            part[half, first + (j // 2) * (512 // WIRE) + q] = total[:, q * WIRE:(q + 1) * WIRE]

    def put_dec(ar, j, total):
        half = lax.rem(j, 2)
        part_d[ar, half, :, pl.ds(pl.multiple_of((j // 2) * 512, 512), 512)] = total

    def no_comm(i):
        pass

    def norm_rows(first):
        def square(q, acc):
            val = hid[q // per, first + lax.rem(q, per)].astype(jnp.float32)
            val = val * val
            return acc + val
        acc = lax.fori_loop(0, 2 * per, square, jnp.zeros((HALF_ROWS, WIRE), jnp.float32))
        inv = lax.rsqrt(jnp.sum(acc, axis=-1, keepdims=True) / width + NORM_EPS)

        def scale(q, carry):
            cols = pl.ds(pl.multiple_of(q * WIRE, WIRE), WIRE)
            val = hid[q // per, first + lax.rem(q, per)].astype(jnp.float32)
            normed[:, cols] = (val * inv * norm_a_ref[:, cols]).astype(jnp.bfloat16)
            return carry
        lax.fori_loop(0, 2 * per, scale, 0)

    barrier = pltpu.get_barrier_semaphore()
    for step in (-1, 1):
        @pl.when((z + step >= 0) & (z + step <= 3))
        def _():
            pl.semaphore_signal(barrier, inc=1, device_id={'tp': lax.rem(z + 4 + step, 4)}, device_id_type=MESH_ID)

    for slot in range(RING):
        dn_copy(wo_b, slot, slot).start()
    for slot in range(RING):
        ug_copy(wug_a, slot, slot).start()

    pl.semaphore_wait(barrier, jnp.where((z == 0) | (z == 3), 1, 2))

    def dec_proj(j, slot):
        put_dec(0, j, jnp.dot(attn_b_ref[...], dn_buf[slot, :attn_b_ref.shape[1], :], preferred_element_type=jnp.float32))
    dn_phase(wo_b, wo_a, 0, dec_proj, no_comm)

    def prompt_proj(j, slot):
        total = jnp.dot(attn_a_ref[...], dn_buf[slot, :attn_a_ref.shape[1], :], preferred_element_type=jnp.float32)
        put_part(j, 0, total[:HALF_ROWS])
        put_part(j, per, total[HALF_ROWS:])
    dn_phase(wo_a, wd_a, n_dn, prompt_proj, no_comm)

    depth = 6 * SKEW
    flow_one = (0, 2 * per, False, 0)
    dec_two = per + n_up + n_dn
    flow_c0 = (2 * per, 3 * per, True, dec_two)
    flow_c1 = (2 * per, 4 * per, True, dec_two)

    def slots(first, last, flow):
        def at(s, carry):
            slot_step(s, *flow)
            return carry
        lax.fori_loop(first, last, at, 0)

    def beside(first, count, flow):
        def at(i):
            @pl.when(i < count)
            def _():
                slot_step(first + i, *flow)
        return at

    slots(0, per + depth, flow_one)

    norm_rows(0)
    rest = per
    up_phase(wug_a, wug_a, 0, normed, act, beside(per + depth, n_up, flow_one))
    dn_phase(wd_a, wd_a, 2 * n_dn, lambda j, slot: put_part(j, 2 * per, down_dot(act, slot)), beside(per + depth + n_up, rest - n_up, flow_one))

    norm_rows(per)
    up_phase(wug_a, wug_b, n_up, normed, act, beside(0, n_up, flow_c0))
    dn_phase(wd_a, wd_b, 3 * n_dn, lambda j, slot: put_part(j, 3 * per, down_dot(act, slot)), beside(n_up, per - n_up, flow_c0))

    val = jnp.concatenate([hid_d[0, 0], hid_d[0, 1]], axis=-1).astype(jnp.float32)
    inv = lax.rsqrt(jnp.mean(val * val, axis=-1, keepdims=True) + NORM_EPS)
    normed_d[...] = (val * inv * norm_b_ref[...]).astype(jnp.bfloat16)
    up_phase(wug_b, None, 2 * n_up, normed_d, act_d, beside(per, n_up, flow_c1))
    dn_phase(wd_b, None, 4 * n_dn, lambda j, slot: put_dec(1, j, down_dot(act_d, slot)), beside(per + n_up, n_dn, flow_c1))
    slots(dec_two, max(2 * per, dec_two + 1) + depth, flow_c1)

    out_b[:, :mid] = hid_d[1, 0]
    out_b[:, mid:] = hid_d[1, 1]

    for half in range(2):
        for ar in range(2):
            @pl.when(pos(half) < 3)
            def _():
                rsd_copy(ar, half).wait_send()

            @pl.when(pos(half) > 0)
            def _():
                agd_copy(ar, half).wait_send()

    for half in range(2):
        @pl.when(pos(half) < 3)
        def _():
            remote(part.at[half], rcv.at[half], rs_send.at[half], rs_recv.at[half, 0], fwd(half)).wait_send()

        @pl.when(pos(half) > 0)
        def _():
            remote(hid.at[half], hid.at[half], ag_send.at[half], ag_recv.at[half, 0], bwd(half)).wait_send()
        pltpu.make_async_copy(hid.at[half, pl.ds(0, 2 * per)], hid.at[half, pl.ds(2 * per, 2 * per)], out_sem.at[half]).wait()


def block_call(x_rows, y_rows, attn_a, attn_b, norm_a, norm_b, wo_a, wug_a, wd_a, wo_b, wug_b, wd_b):
    rows, width = x_rows.shape
    dec_rows = y_rows.shape[0]
    ffn = wd_a.shape[0]
    mid = width // 2
    per = mid // WIRE
    n_up = -(-ffn // COLS)
    vmem = pl.BlockSpec(memory_space=pltpu.VMEM)
    hbm = pl.BlockSpec(memory_space=pl.ANY)
    dma = pltpu.SemaphoreType.DMA
    weights = 2 * (wo_a.size + wug_a.size + wd_a.size)
    return pl.pallas_call(
        block_kernel,
        out_shape=(jax.ShapeDtypeStruct((rows, width), jnp.bfloat16), jax.ShapeDtypeStruct((dec_rows, width), jnp.bfloat16)),
        in_specs=[vmem] * 6 + [hbm] * 6,
        out_specs=(hbm, vmem),
        scratch_shapes=[
            pltpu.VMEM((2, 4 * per, HALF_ROWS, WIRE), jnp.float32),
            pltpu.VMEM((2, 4 * per, HALF_ROWS, WIRE), jnp.float32),
            pltpu.VMEM((2, 4 * per, HALF_ROWS, WIRE), jnp.bfloat16),
            pltpu.VMEM((2, 2, dec_rows, mid), jnp.float32),
            pltpu.VMEM((2, 2, dec_rows, mid), jnp.float32),
            pltpu.VMEM((2, 2, dec_rows, mid), jnp.bfloat16),
            pltpu.VMEM((HALF_ROWS, width), jnp.bfloat16),
            pltpu.VMEM((n_up, HALF_ROWS, COLS), jnp.bfloat16),
            pltpu.VMEM((dec_rows, width), jnp.bfloat16),
            pltpu.VMEM((n_up, dec_rows, COLS), jnp.bfloat16),
            pltpu.VMEM((RING, 2, COLS, width), jnp.bfloat16),
            pltpu.VMEM((RING, ffn, 512), jnp.bfloat16),
            dma((2,)), dma((2, 4 * per)), dma((2,)), dma((2, 4 * per)),
            dma((2, 2)), dma((2, 2)), dma((2, 2)), dma((2, 2)),
            dma((RING,)), dma((RING,)), dma((2,)),
        ],
        compiler_params=pltpu.CompilerParams(collective_id=0, has_side_effects=True, vmem_limit_bytes=62 * 1024 * 1024),
        cost_estimate=pl.CostEstimate(flops=weights * (rows + dec_rows) // 2, bytes_accessed=weights * 3, transcendentals=0),
        name='block',
    )(x_rows, y_rows, attn_a, attn_b, norm_a, norm_b, wo_a, wug_a, wd_a, wo_b, wug_b, wd_b)


def prefill_attention(x_rows, seq_len, w_qkv, head_dim, gain):
    num_rows = x_rows.shape[0]
    kv_loc = w_qkv.shape[1]
    group = w_qkv.shape[2] // head_dim - 2
    positions = jnp.arange(num_rows)
    normed = rms_norm(x_rows, gain)
    qkv_all = jnp.einsum('sd,dhe->she', normed, w_qkv, preferred_element_type=jnp.float32).astype(jnp.bfloat16)
    qkv_all = qkv_all.reshape(num_rows, kv_loc, group + 2, head_dim)
    queries = rope_rot(qkv_all[:, :, :group], positions)
    keys = rope_rot(qkv_all[:, :, group], positions)
    vals = qkv_all[:, :, group + 1]
    allowed = (positions[None, :] <= positions[:, None]) & (positions[None, :] < seq_len)
    scores = jnp.einsum('qhgd,khd->hgqk', queries, keys, preferred_element_type=jnp.float32) * head_dim ** -0.5
    scores = jnp.where(allowed, scores, -1e30)
    attn_prob = jax.nn.softmax(scores, axis=-1).astype(jnp.bfloat16)
    attn_out = jnp.einsum('hgqk,khd->qhgd', attn_prob, vals, preferred_element_type=jnp.float32).astype(jnp.bfloat16)
    valid = (positions < seq_len)[:, None, None]
    zero_val = jnp.zeros((), jnp.bfloat16)
    return attn_out.reshape(num_rows, kv_loc * group * head_dim), jnp.where(valid, keys, zero_val), jnp.where(valid, vals, zero_val)


def decode_attention(tokens, lengths, k_cache, v_cache, w_qkv, head_dim, gain):
    batch_rows = tokens.shape[0]
    kv_loc = w_qkv.shape[1]
    tp_loc = w_qkv.shape[2]
    group = w_qkv.shape[3] // head_dim - 2
    slot_pos = jnp.arange(k_cache.shape[1])
    write_slot = (slot_pos[None, :] == lengths[:, None])[:, :, None, None, None]
    visible = (slot_pos[None, :] <= lengths[:, None])[:, None, None, None, :]
    normed = rms_norm(tokens, gain)
    qkv_all = jnp.einsum('bd,dije->bije', normed, w_qkv, preferred_element_type=jnp.float32).astype(jnp.bfloat16)
    qkv_all = qkv_all.reshape(batch_rows, kv_loc, tp_loc, group + 2, head_dim)
    queries = rope_rot(qkv_all[:, :, :, :group], lengths)
    key_new = rope_rot(qkv_all[:, :, :, group], lengths)
    val_new = qkv_all[:, :, :, group + 1]
    key_upd = jnp.where(write_slot, key_new[:, None], k_cache)
    val_upd = jnp.where(write_slot, val_new[:, None], v_cache)
    scores = jnp.einsum('bijge,bsije->bijgs', queries, key_upd, preferred_element_type=jnp.float32) * head_dim ** -0.5
    scores = jnp.where(visible, scores, -1e30)
    attn_prob = jax.nn.softmax(scores, axis=-1).astype(jnp.bfloat16)
    attn_out = jnp.einsum('bijgs,bsije->bijge', attn_prob, val_upd, preferred_element_type=jnp.float32).astype(jnp.bfloat16)
    return attn_out.reshape(batch_rows, kv_loc * tp_loc * group * head_dim), key_upd, val_upd


def hand_off(keys, vals, tp_size, side_size):
    num_rows, heads, head_dim = keys.shape
    fold = heads // tp_size
    both = jnp.stack([keys, vals]).reshape(2, num_rows, fold, tp_size, head_dim)
    tp_idx = lax.axis_index('tp')
    out = jnp.zeros((2, num_rows, tp_size, fold, head_dim), keys.dtype)
    for step in range(tp_size):
        piece = lax.dynamic_index_in_dim(both, (tp_idx + step) % tp_size, axis=3, keepdims=False)
        pairs = [(src * side_size + side, ((src + step) % tp_size) * side_size + (side + side_size // 2) % side_size)
                 for src in range(tp_size) for side in range(side_size)]
        moved = lax.ppermute(piece, ('tp', 'side'), pairs)
        out = lax.dynamic_update_index_in_dim(out, moved, (tp_idx - step) % tp_size, axis=2)
    out = out.reshape(2, 1, num_rows, heads, 1, head_dim)
    return out[0], out[1]


def solution(mesh):
    tp_size = mesh.shape['tp']
    side_size = mesh.shape['side']
    rows_spec = P(('pair', 'side'), None)
    flat_spec = P(('pair', 'side'))
    cache_spec = P(None, ('pair', 'side'), None, None, 'tp', None)
    prompt_spec = P(None, ('pair', 'side'), None, 'tp', None)
    in_specs = (rows_spec, flat_spec, rows_spec, cache_spec, cache_spec, flat_spec,
                P(None, None, 'tp', None), P(None, 'tp', None, None), P(None, None, None, 'tp'), P(None, 'tp', None), P(),
                P(None, None, None, 'tp', None), P(None, None, 'tp', None, None), P(None, None, None, 'tp'), P(None, 'tp', None), P())
    out_specs = (rows_spec, rows_spec, prompt_spec, prompt_spec, cache_spec, cache_spec)

    def body(x_prompt, s_len, y_tok, k_cache, v_cache, c_len, wqkv_a, wo_a, wug_a, wd_a, norm_a, wqkv_b, wo_b, wug_b, wd_b, norm_b):
        width = x_prompt.shape[1]
        head_dim = k_cache.shape[-1]
        attn_a, keys, vals = prefill_attention(x_prompt, s_len[0], wqkv_a[0], head_dim, norm_a[0, 0])
        k_prompt, v_prompt = hand_off(keys, vals, tp_size, side_size)
        attn_b, k_new, v_new = decode_attention(y_tok, c_len, k_cache[0], v_cache[0], wqkv_b[0], head_dim, norm_b[0, 0])
        hidden, y_out = block_call(
            x_prompt, y_tok, attn_a, attn_b, norm_a[0, 1:2].astype(jnp.float32), norm_b[0, 1:2].astype(jnp.float32),
            wo_a[0].reshape(-1, width), jnp.transpose(wug_a[0], (1, 2, 0)), wd_a[0],
            wo_b[0].reshape(-1, width), jnp.transpose(wug_b[0], (1, 2, 0)), wd_b[0])
        return hidden, y_out, k_prompt, v_prompt, k_new[None], v_new[None]

    return jax.shard_map(body, mesh=mesh, in_specs=in_specs, out_specs=out_specs, check_vma=False)
```

time: 532 us -> 293 us (0.55); the launches traced: 523 us -> 292 us
  blocking collectives: 297 us -> 0 us
  Pallas kernels: 0 us -> 198 us
  matrix products: 156 us -> 36.3 us
  waiting for transfers between devices: 7.57 us -> 0.01 us
  other arithmetic: 36.1 us -> 29.8 us
    psum x2 -> x0, blocking collectives: 297 us -> none  [tp_sum(): return lax.psum(part_sum, 'tp')]
    pallas_call x0 -> x1, Pallas kernels: none -> 198 us  [block_call(): pl.pallas_call(block_kernel, out_shape=(jax.ShapeDtypeStruct((rows, width...]
    dot_general x16 -> x6, matrix products: 156 us -> 36.3 us  [the longest x1 17.4 us: prefill_attention(): jnp.einsum('sd,dhe->she', normed, w_qkv, preferred_element_type=jnp.float32)]
    all_to_all x2 -> x0, waiting for transfers between devices: 7.57 us -> none  [tp_relayout(): return lax.all_to_all(split_view, 'tp', 3, 2, tiled=True)]
    all_to_all x2 -> x0, starting transfers between devices: 7.55 us -> none  [tp_relayout(): return lax.all_to_all(split_view, 'tp', 3, 2, tiled=True)]
    ppermute x2 -> x4, starting transfers between devices: 3.06 us -> 9.37 us  [hand_off(): moved = lax.ppermute(piece, ('tp', 'side'), pairs)]
    dynamic_update_slice x0 -> x4, local copies, waits for them, and re-layouts: none -> 5.7 us  [hand_off(): lax.dynamic_update_index_in_dim(out, moved, (tp_idx - step) % tp_size, ax...]
  transfers between devices with their start and end apart: 4 -> 4, of which waited for: 1 -> 0; matrix products, arithmetic and copies ran while one was open for 31% -> 17% of each run, Pallas kernels for 0% -> 68%
where the time goes in v1:
time: 293 us; the launch traced here: 292 us
  Pallas kernels  198 us (68%)
  matrix products  36.3 us (12%)
  other arithmetic  29.8 us (10%)
  local copies, waits for them, and re-layouts  17.1 us (6%)
  starting transfers between devices  9.37 us (3%)
    pallas_call x1, Pallas kernels, block_call(): pl.pallas_call(block_kernel, out_shape=(jax.ShapeDtypeStruct((rows, width...  198 us
    dot_general x1, matrix products, prefill_attention(): jnp.einsum('sd,dhe->she', normed, w_qkv, preferred_element_type=jnp.float32)  17.4 us
    dot_general x1, matrix products, decode_attention(): jnp.einsum('bd,dije->bije', normed, w_qkv, preferred_element_type=jnp.flo...  13.5 us
    select_n x1, other arithmetic, decode_attention(): val_upd = jnp.where(write_slot, val_new[:, None], v_cache)  9.8 us
    ppermute x4, starting transfers between devices, hand_off(): moved = lax.ppermute(piece, ('tp', 'side'), pairs)  9.37 us
    select_n x1, other arithmetic, decode_attention(): key_upd = jnp.where(write_slot, key_new[:, None], k_cache)  8.49 us
  transfers between devices with their start and end apart: 4, of which 0 were waited for; matrix products, arithmetic and copies ran while one was open for 17% of the time, Pallas kernels for 68%

profile of v1, /device:TPU:0, one launch (start us, length us, event | category | flops | bytes accessed | tf_op | source)
XLA Modules:
  0.0 292.1 jit_solution(683714978699895404)
XLA Ops:
  0.7 2.1 fusion.6
  2.8 1.5 bitcast_convert_fusion.1
  4.3 17.4 %fusion.18 = bf16[256,8,384]{2,0,1:T(8,128)(2,1)} fusion(bf16[4096,8,384]{2,1,0:T(8,128)(2,1)} %bitcast.157, bf16[256,4096]{1,0:T(8,128)(2,1)} %x_ref.1, f32[4096]{0:T(1024)S(1)} %bitcast.156, f32[256]{0:T(256)S(1)} %add_rsqrt_fusion), kind=kOutput, calls=%fused_computation.26 | convolution fusion | flops 6447431680 | bytes 28853248 | tf_op jit(solution)/shard_map/sd,dhe->she/dot_general | solution.py:361
  21.7 2.3 copy.134
  26.8 1.7 broadcast_select_fusion.2
  29.5 3.0 %collective-permute-start = (bf16[2,256,2,128]{3,1,2,0:T(8,128)(2,1)}, bf16[2,256,2,128]{3,1,2,0:T(8,128)(2,1)}, u32[]{:S(2)}, u32[]{:S(2)}) collective-permute-start(bf16[2,256,2,128]{3,1,2,0:T(8,128)(2,1)} %get-tuple-element.19), channel_id=1, source_target_pairs={{0,2},{1,3},{2,0},{3,1},{4,6},{5,7},{6,4},{7,5},{8,10},{9,11},{10,... | collective-permute-start | bytes 786440 | tf_op jit(solution)/shard_map/ppermute | solution.py:409
  32.5 1.5 collective-permute-start.1
  34.1 3.5 %collective-permute-start.2 = (bf16[2,256,2,128]{3,1,2,0:T(8,128)(2,1)}, bf16[2,256,2,128]{3,1,2,0:T(8,128)(2,1)}, u32[]{:S(2)}, u32[]{:S(2)}) collective-permute-start(bf16[2,256,2,128]{3,1,2,0:T(8,128)(2,1)} %get-tuple-element.21), channel_id=1, source_target_pairs={{0,10},{1,11},{2,8},{3,9},{4,14},{5,15},{6,12},{7,13},{8,2},{9,3},... | collective-permute-start | bytes 786440 | tf_op jit(solution)/shard_map/ppermute | solution.py:409
  37.6 1.3 collective-permute-start.3
  38.9 1.0 fusion.95
  40.7 1.1 copy.91
  42.5 1.3 iota_compare_fusion.2
  44.0 13.5 %fusion.29 = bf16[8,8,1,3,128]{4,0,3,1,2:T(8,128)(2,1)S(1)} fusion(bf16[4096,8,384]{2,1,0:T(8,128)(2,1)} %bitcast.140, bf16[8,4096]{1,0:T(8,128)(2,1)S(1)} %copy-done.4, f32[4096]{0:T(1024)S(1)} %bitcast.154, f32[8]{0:T(128)S(1)} %add_rsqrt_fusion.1), kind=kOutput, calls=%fused_computation.49 | convolution fusion | flops 201482240 | bytes 25296928 | tf_op jit(solution)/shard_map/bd,dije->bije/dot_general | solution.py:385
  61.2 8.5 %bitcast_select_fusion.1 = (bf16[8,256,8,128]{3,2,1,0:T(8,128)(2,1)S(1)}, bf16[8,256,8,128]{3,2,1,0:T(8,128)(2,1)}) fusion(bf16[1,8,256,8,1,128]{5,3,4,2,1,0:T(8,128)(2,1)} %param.19, pred[8,256]{1,0:T(8,128)(4,1)S(1)} %copy-done.7, bf16[8,8,128]{2,1,0:T(8,128)(2,1)S(1)} %copy.74, bf16[1,8,256,8,1,128]{5,3,4,2,1,0:T(8,128)(2,1)} %param.20, ...), kind=kLoop, calls=%fused_computation.12 | loop fusion | flops 4194304 | bytes 16812032 | tf_op jit(solution)/shard_map/jit(_where)/select_n | solution.py:390
  69.7 1.2 fusion.11
  71.0 2.8 fusion.9
  74.5 197.8 %block.1 = (bf16[256,4096]{1,0:T(8,128)(2,1)}, bf16[8,4096]{1,0:T(8,128)(2,1)}) custom-call(bf16[256,4096]{1,0:T(8,128)(2,1)} %x_ref.1, bf16[8,4096]{1,0:T(8,128)(2,1)} %y_ref.1, bf16[256,1024]{1,0:T(8,128)(2,1)} %copy.90.attn_a_ref, bf16[8,1024]{1,0:T(8,128)(2,1)} %bitcast.155, f32[1,4096]{1,0:T(1,128)} %get-tuple-element.47.norm_a_ref, ...), custom_call_target="tpu_custom_call" | custom-call | flops 10034872320 | bytes 228065280 | tf_op jit(solution)/shard_map/block/pallas_call | solution.py:327
  272.4 9.8 %broadcast_select_fusion = (bf16[1,8,256,8,1,128]{5,3,4,2,1,0:T(8,128)(2,1)}, bf16[1,8,256,8,1,128]{5,3,4,2,1,0:T(8,128)(2,1)}) fusion(bf16[1,8,256,8,1,128]{5,3,4,2,1,0:T(8,128)(2,1)} %param.20, pred[8,256]{1,0:T(8,128)(4,1)S(1)} %copy-done.7, bf16[8,8,128]{2,1,0:T(8,128)(2,1)S(1)} %copy.75, bf16[1,8,256,8,1,128]{5,3,4,2,1,0:T(8,128)(2,1)} %param.19, ...), kind=kLoop, calls=%fused_computation.17 | loop fusion | flops 4194304 | bytes 16812032 | tf_op jit(solution)/shard_map/jit(_where)/select_n | solution.py:391
  282.7 1.5 copy_dynamic-update-slice_fusion.3
  284.2 1.4 copy_dynamic-update-slice_fusion.2
  285.6 1.4 copy_dynamic-update-slice_fusion.1
  287.1 1.4 copy_dynamic-update-slice_fusion
  288.5 1.7 fusion.96
  290.2 1.3 copy.144
  (60 shorter events, 10.3 us)
Async XLA Ops:
  0.7 25.1 %copy-start.8 = (f32[64]{0:T(128)}, f32[64]{0:T(128)S(1)}, u32[]{:S(2)}) copy-start(f32[64]{0:T(128)S(1)} %multiply_power_fusion) | copy-start | bytes 772
  25.7 13.1 %copy-start.11 = (pred[256]{0:T(512)(128)(4,1)}, pred[256]{0:T(512)(128)(4,1)S(1)}, u32[]{:S(2)}) copy-start(pred[256]{0:T(512)(128)(4,1)S(1)} %iota_compare_fusion.3) | copy-start | bytes 772
  26.8 13.2 %copy-start = (bf16[256,8,64]{2,0,1:T(8,128)(2,1)}, bf16[256,8,64]{2,0,1:T(8,128)(2,1)S(1)}, u32[]{:S(2)}) copy-start(bf16[256,8,64]{2,0,1:T(8,128)(2,1)S(1)} %get-tuple-element.23) | copy-start | bytes 786436
  26.8 17.0 %copy-start.4 = (bf16[8,4096]{1,0:T(8,128)(2,1)S(1)}, bf16[8,4096]{1,0:T(8,128)(2,1)}, u32[]{:S(2)}) copy-start(bf16[8,4096]{1,0:T(8,128)(2,1)} %y_ref.1) | copy-start | bytes 196612
  29.5 252.7 %collective-permute-start = (bf16[2,256,2,128]{3,1,2,0:T(8,128)(2,1)}, bf16[2,256,2,128]{3,1,2,0:T(8,128)(2,1)}, u32[]{:S(2)}, u32[]{:S(2)}) collective-permute-start(bf16[2,256,2,128]{3,1,2,0:T(8,128)(2,1)} %get-tuple-element.19), channel_id=1, source_target_pairs={{0,2},{1,3},{2,0},{3,1},{4,6},{5,7},{6,4},{7,5},{8,10},{9,11},{10,... | collective-permute-start | bytes 786440 | tf_op jit(solution)/shard_map/ppermute | solution.py:409
  32.5 251.7 %collective-permute-start.1 = (bf16[2,256,2,128]{3,1,2,0:T(8,128)(2,1)}, bf16[2,256,2,128]{3,1,2,0:T(8,128)(2,1)}, u32[]{:S(2)}, u32[]{:S(2)}) collective-permute-start(bf16[2,256,2,128]{3,1,2,0:T(8,128)(2,1)} %get-tuple-element.20), channel_id=1, source_target_pairs={{0,6},{1,7},{2,4},{3,5},{4,10},{5,11},{6,8},{7,9},{8,14},{9,15},{1... | collective-permute-start | bytes 786440 | tf_op jit(solution)/shard_map/ppermute | solution.py:409
  34.1 251.6 %collective-permute-start.2 = (bf16[2,256,2,128]{3,1,2,0:T(8,128)(2,1)}, bf16[2,256,2,128]{3,1,2,0:T(8,128)(2,1)}, u32[]{:S(2)}, u32[]{:S(2)}) collective-permute-start(bf16[2,256,2,128]{3,1,2,0:T(8,128)(2,1)} %get-tuple-element.21), channel_id=1, source_target_pairs={{0,10},{1,11},{2,8},{3,9},{4,14},{5,15},{6,12},{7,13},{8,2},{9,3},... | collective-permute-start | bytes 786440 | tf_op jit(solution)/shard_map/ppermute | solution.py:409
  37.6 249.5 %collective-permute-start.3 = (bf16[2,256,2,128]{3,1,2,0:T(8,128)(2,1)}, bf16[2,256,2,128]{3,1,2,0:T(8,128)(2,1)}, u32[]{:S(2)}, u32[]{:S(2)}) collective-permute-start(bf16[2,256,2,128]{3,1,2,0:T(8,128)(2,1)} %get-tuple-element.18), channel_id=1, source_target_pairs={{0,14},{1,15},{2,12},{3,13},{4,2},{5,3},{6,0},{7,1},{8,6},{9,7},{1... | collective-permute-start | bytes 786440 | tf_op jit(solution)/shard_map/ppermute | solution.py:409
  43.9 13.5 %copy-start.9 = (f32[64]{0:T(128)S(1)}, f32[64]{0:T(128)}, u32[]{:S(2)}) copy-start(f32[64]{0:T(128)} %copy-done.8) | copy-start | bytes 772
  44.0 13.8 %copy-start.3 = (bf16[256,8,1,64]{3,1,2,0:T(8,128)(2,1)S(1)}, bf16[256,8,1,64]{3,1,2,0:T(8,128)(2,1)}, u32[]{:S(2)}) copy-start(bf16[256,8,1,64]{3,1,2,0:T(8,128)(2,1)} %get-tuple-element.13) | copy-start | bytes 786436
  44.0 14.2 %copy-start.1 = (bf16[256,8,64]{2,0,1:T(8,128)(2,1)S(1)}, bf16[256,8,64]{2,0,1:T(8,128)(2,1)}, u32[]{:S(2)}) copy-start(bf16[256,8,64]{2,0,1:T(8,128)(2,1)} %copy-done) | copy-start | bytes 786436
  57.8 1.5 copy-start.5
  59.3 1.9 copy-start.7
  69.7 1.2 copy-start.10
  282.2 8.0 %copy-start.2 = (bf16[256,4096]{1,0:T(8,128)(2,1)S(1)}, bf16[256,4096]{1,0:T(8,128)(2,1)}, u32[]{:S(2)}) copy-start(bf16[256,4096]{1,0:T(8,128)(2,1)} %get-tuple-element.54) | copy-start | bytes 6291460
  282.7 8.8 %copy-start.6 = (bf16[8,4096]{1,0:T(8,128)(2,1)S(1)}, bf16[8,4096]{1,0:T(8,128)(2,1)}, u32[]{:S(2)}) copy-start(bf16[8,4096]{1,0:T(8,128)(2,1)} %get-tuple-element.55) | copy-start | bytes 196612

commit v2 on v1

--- a/solution.py
+++ b/solution.py
@@ -32,13 +32,14 @@
 HALF_ROWS = 128
 RING = 3
 WIRE = 128
+FRONT_RING = 4
 SKEW = 2
 
 
-def block_kernel(x_ref, y_ref, attn_a_ref, attn_b_ref, norm_a_ref, norm_b_ref, wo_a, wug_a, wd_a, wo_b, wug_b, wd_b,
-                 out_a, out_b,
+def block_kernel(x_ref, y_ref, attn_a_ref, attn_b_ref, norm_a_ref, norm_b_ref, wo_a, wug_a, wd_a, wo_b, wug_b, wd_b, keys, vals,
+                 out_a, out_b, k_out, v_out,
                  part, rcv, hid, part_d, rcv_d, hid_d, normed, act, normed_d, act_d, ug_buf, dn_buf,
-                 rs_send, rs_recv, ag_send, ag_recv, rsd_send, rsd_recv, agd_send, agd_recv, ug_sem, dn_sem, out_sem):
+                 rs_send, rs_recv, ag_send, ag_recv, rsd_send, rsd_recv, agd_send, agd_recv, ug_sem, dn_sem, out_sem, hand_send, hand_recv):
     ffn, width = wd_a.shape
     mid = width // 2
     per = mid // WIRE
@@ -229,7 +230,22 @@
             return carry
         lax.fori_loop(0, 2 * per, scale, 0)
 
+    side = lax.axis_index('side')
+    n_side = lax.axis_size('side')
+    there = lax.rem(side + n_side // 2, n_side)
+
+    def hand_copy(which, step):
+        dest = lax.rem(z + step, 4)
+        src, dst = ((keys, k_out), (vals, v_out))[which]
+        fold = src.shape[2]
+        return pltpu.make_async_remote_copy(
+            src_ref=src.at[dest], dst_ref=dst.at[:, pl.ds(pl.multiple_of(z * fold, fold), fold)],
+            send_sem=hand_send.at[which, step], recv_sem=hand_recv.at[which, step],
+            device_id={'tp': dest, 'side': there}, device_id_type=MESH_ID)
+
     barrier = pltpu.get_barrier_semaphore()
+    for step in range(4):
+        pl.semaphore_signal(barrier, inc=1, device_id={'tp': lax.rem(z + step, 4), 'side': there}, device_id_type=MESH_ID)
     for step in (-1, 1):
         @pl.when((z + step >= 0) & (z + step <= 3))
         def _():
@@ -240,7 +256,9 @@
     for slot in range(RING):
         ug_copy(wug_a, slot, slot).start()
 
-    pl.semaphore_wait(barrier, jnp.where((z == 0) | (z == 3), 1, 2))
+    pl.semaphore_wait(barrier, jnp.where((z == 0) | (z == 3), 5, 6))
+    for step in range(4):
+        hand_copy(0, step).start()
 
     def dec_proj(j, slot):
         put_dec(0, j, jnp.dot(attn_b_ref[...], dn_buf[slot, :attn_b_ref.shape[1], :], preferred_element_type=jnp.float32))
@@ -272,15 +290,17 @@
         return at
 
     slots(0, per + depth, flow_one)
+    for step in range(4):
+        hand_copy(1, step).start()
 
     norm_rows(0)
-    rest = per
-    up_phase(wug_a, wug_a, 0, normed, act, beside(per + depth, n_up, flow_one))
-    dn_phase(wd_a, wd_a, 2 * n_dn, lambda j, slot: put_part(j, 2 * per, down_dot(act, slot)), beside(per + depth + n_up, rest - n_up, flow_one))
+    lead = min(n_up, per)
+    up_phase(wug_a, wug_a, 0, normed, act, beside(per + depth, lead, flow_one))
+    dn_phase(wd_a, wd_a, 2 * n_dn, lambda j, slot: put_part(j, 2 * per, down_dot(act, slot)), beside(per + depth + lead, per - lead, flow_one))
 
     norm_rows(per)
-    up_phase(wug_a, wug_b, n_up, normed, act, beside(0, n_up, flow_c0))
-    dn_phase(wd_a, wd_b, 3 * n_dn, lambda j, slot: put_part(j, 3 * per, down_dot(act, slot)), beside(n_up, per - n_up, flow_c0))
+    up_phase(wug_a, wug_b, n_up, normed, act, beside(0, lead, flow_c0))
+    dn_phase(wd_a, wd_b, 3 * n_dn, lambda j, slot: put_part(j, 3 * per, down_dot(act, slot)), beside(lead, per - lead, flow_c0))
 
     val = jnp.concatenate([hid_d[0, 0], hid_d[0, 1]], axis=-1).astype(jnp.float32)
     inv = lax.rsqrt(jnp.mean(val * val, axis=-1, keepdims=True) + NORM_EPS)
@@ -289,6 +309,9 @@
     dn_phase(wd_b, None, 4 * n_dn, lambda j, slot: put_dec(1, j, down_dot(act_d, slot)), beside(per + n_up, n_dn, flow_c1))
     slots(dec_two, max(2 * per, dec_two + 1) + depth, flow_c1)
 
+    for which in range(2):
+        for step in range(4):
+            hand_copy(which, step).wait()
     out_b[:, :mid] = hid_d[1, 0]
     out_b[:, mid:] = hid_d[1, 1]
 
@@ -313,7 +336,7 @@
         pltpu.make_async_copy(hid.at[half, pl.ds(0, 2 * per)], hid.at[half, pl.ds(2 * per, 2 * per)], out_sem.at[half]).wait()
 
 
-def block_call(x_rows, y_rows, attn_a, attn_b, norm_a, norm_b, wo_a, wug_a, wd_a, wo_b, wug_b, wd_b):
+def block_call(x_rows, y_rows, attn_a, attn_b, norm_a, norm_b, wo_a, wug_a, wd_a, wo_b, wug_b, wd_b, keys, vals):
     rows, width = x_rows.shape
     dec_rows = y_rows.shape[0]
     ffn = wd_a.shape[0]
@@ -326,9 +349,10 @@
     weights = 2 * (wo_a.size + wug_a.size + wd_a.size)
     return pl.pallas_call(
         block_kernel,
-        out_shape=(jax.ShapeDtypeStruct((rows, width), jnp.bfloat16), jax.ShapeDtypeStruct((dec_rows, width), jnp.bfloat16)),
-        in_specs=[vmem] * 6 + [hbm] * 6,
-        out_specs=(hbm, vmem),
+        out_shape=(jax.ShapeDtypeStruct((rows, width), jnp.bfloat16), jax.ShapeDtypeStruct((dec_rows, width), jnp.bfloat16),
+                   *[jax.ShapeDtypeStruct((rows, keys.shape[0] * keys.shape[2]), jnp.bfloat16)] * 2),
+        in_specs=[vmem] * 6 + [hbm] * 8,
+        out_specs=(hbm, vmem, hbm, hbm),
         scratch_shapes=[
             pltpu.VMEM((2, 4 * per, HALF_ROWS, WIRE), jnp.float32),
             pltpu.VMEM((2, 4 * per, HALF_ROWS, WIRE), jnp.float32),
@@ -344,72 +368,173 @@
             pltpu.VMEM((RING, ffn, 512), jnp.bfloat16),
             dma((2,)), dma((2, 4 * per)), dma((2,)), dma((2, 4 * per)),
             dma((2, 2)), dma((2, 2)), dma((2, 2)), dma((2, 2)),
-            dma((RING,)), dma((RING,)), dma((2,)),
+            dma((RING,)), dma((RING,)), dma((2,)), dma((2, 4)), dma((2, 4)),
         ],
         compiler_params=pltpu.CompilerParams(collective_id=0, has_side_effects=True, vmem_limit_bytes=62 * 1024 * 1024),
         cost_estimate=pl.CostEstimate(flops=weights * (rows + dec_rows) // 2, bytes_accessed=weights * 3, transcendentals=0),
         name='block',
-    )(x_rows, y_rows, attn_a, attn_b, norm_a, norm_b, wo_a, wug_a, wd_a, wo_b, wug_b, wd_b)
-
-
-def prefill_attention(x_rows, seq_len, w_qkv, head_dim, gain):
-    num_rows = x_rows.shape[0]
-    kv_loc = w_qkv.shape[1]
-    group = w_qkv.shape[2] // head_dim - 2
-    positions = jnp.arange(num_rows)
-    normed = rms_norm(x_rows, gain)
-    qkv_all = jnp.einsum('sd,dhe->she', normed, w_qkv, preferred_element_type=jnp.float32).astype(jnp.bfloat16)
-    qkv_all = qkv_all.reshape(num_rows, kv_loc, group + 2, head_dim)
-    queries = rope_rot(qkv_all[:, :, :group], positions)
-    keys = rope_rot(qkv_all[:, :, group], positions)
-    vals = qkv_all[:, :, group + 1]
-    allowed = (positions[None, :] <= positions[:, None]) & (positions[None, :] < seq_len)
-    scores = jnp.einsum('qhgd,khd->hgqk', queries, keys, preferred_element_type=jnp.float32) * head_dim ** -0.5
-    scores = jnp.where(allowed, scores, -1e30)
-    attn_prob = jax.nn.softmax(scores, axis=-1).astype(jnp.bfloat16)
-    attn_out = jnp.einsum('hgqk,khd->qhgd', attn_prob, vals, preferred_element_type=jnp.float32).astype(jnp.bfloat16)
-    valid = (positions < seq_len)[:, None, None]
-    zero_val = jnp.zeros((), jnp.bfloat16)
-    return attn_out.reshape(num_rows, kv_loc * group * head_dim), jnp.where(valid, keys, zero_val), jnp.where(valid, vals, zero_val)
-
-
-def decode_attention(tokens, lengths, k_cache, v_cache, w_qkv, head_dim, gain):
-    batch_rows = tokens.shape[0]
-    kv_loc = w_qkv.shape[1]
-    tp_loc = w_qkv.shape[2]
-    group = w_qkv.shape[3] // head_dim - 2
-    slot_pos = jnp.arange(k_cache.shape[1])
-    write_slot = (slot_pos[None, :] == lengths[:, None])[:, :, None, None, None]
-    visible = (slot_pos[None, :] <= lengths[:, None])[:, None, None, None, :]
-    normed = rms_norm(tokens, gain)
-    qkv_all = jnp.einsum('bd,dije->bije', normed, w_qkv, preferred_element_type=jnp.float32).astype(jnp.bfloat16)
-    qkv_all = qkv_all.reshape(batch_rows, kv_loc, tp_loc, group + 2, head_dim)
-    queries = rope_rot(qkv_all[:, :, :, :group], lengths)
-    key_new = rope_rot(qkv_all[:, :, :, group], lengths)
-    val_new = qkv_all[:, :, :, group + 1]
-    key_upd = jnp.where(write_slot, key_new[:, None], k_cache)
-    val_upd = jnp.where(write_slot, val_new[:, None], v_cache)
-    scores = jnp.einsum('bijge,bsije->bijgs', queries, key_upd, preferred_element_type=jnp.float32) * head_dim ** -0.5
-    scores = jnp.where(visible, scores, -1e30)
-    attn_prob = jax.nn.softmax(scores, axis=-1).astype(jnp.bfloat16)
-    attn_out = jnp.einsum('bijgs,bsije->bijge', attn_prob, val_upd, preferred_element_type=jnp.float32).astype(jnp.bfloat16)
-    return attn_out.reshape(batch_rows, kv_loc * tp_loc * group * head_dim), key_upd, val_upd
-
-
-def hand_off(keys, vals, tp_size, side_size):
-    num_rows, heads, head_dim = keys.shape
-    fold = heads // tp_size
-    both = jnp.stack([keys, vals]).reshape(2, num_rows, fold, tp_size, head_dim)
-    tp_idx = lax.axis_index('tp')
-    out = jnp.zeros((2, num_rows, tp_size, fold, head_dim), keys.dtype)
-    for step in range(tp_size):
-        piece = lax.dynamic_index_in_dim(both, (tp_idx + step) % tp_size, axis=3, keepdims=False)
-        pairs = [(src * side_size + side, ((src + step) % tp_size) * side_size + (side + side_size // 2) % side_size)
-                 for src in range(tp_size) for side in range(side_size)]
-        moved = lax.ppermute(piece, ('tp', 'side'), pairs)
-        out = lax.dynamic_update_index_in_dim(out, moved, (tp_idx - step) % tp_size, axis=2)
-    out = out.reshape(2, 1, num_rows, heads, 1, head_dim)
-    return out[0], out[1]
+    )(x_rows, y_rows, attn_a, attn_b, norm_a, norm_b, wo_a, wug_a, wd_a, wo_b, wug_b, wd_b, keys, vals)
+
+
+def front_kernel(s_len, c_len, qkv_a, cos_a, sin_a, slices_b, cos_b, sin_b, wqkv_b, k_cache, v_cache,
+                 attn_a, keys, vals, attn_b, k_new, v_new,
+                 k_buf, v_buf, w_buf, spread, acc, rows_b, k_in, v_in, k_sem, v_sem, w_sem):
+    heads, rows, _ = qkv_a.shape
+    head_dim = cos_a.shape[1]
+    half = head_dim // 2
+    dec_rows, slots_heads, _ = k_cache.shape
+    n_tp = keys.shape[0]
+    depth = w_buf.shape[1]
+    n_w = wqkv_b.shape[0] // depth
+    scale = head_dim ** -0.5
+
+    def w_copy(i, slot):
+        return pltpu.make_async_copy(wqkv_b.at[pl.ds(pl.multiple_of(i * depth, depth), depth), :], w_buf.at[slot], w_sem.at[slot])
+
+    for slot in range(FRONT_RING):
+        w_copy(slot, slot).start()
+
+    def cache_in(b, carry):
+        pltpu.make_async_copy(k_cache.at[b], k_buf.at[b], k_in.at[b]).start()
+        pltpu.make_async_copy(v_cache.at[b], v_buf.at[b], v_in.at[b]).start()
+        return carry
+    lax.fori_loop(0, dec_rows, cache_in, 0)
+
+    def rotate(val, cos_tab, sin_tab):
+        val = val.astype(jnp.float32)
+        swapped = jnp.concatenate([val[:, half:], val[:, :half]], axis=-1)
+        return (val * cos_tab + swapped * sin_tab).astype(jnp.bfloat16)
+
+    row = lax.broadcasted_iota(jnp.int32, (rows, rows), 0)
+    col = lax.broadcasted_iota(jnp.int32, (rows, rows), 1)
+    allowed = (col <= row) & (col < s_len[0])
+    valid = lax.broadcasted_iota(jnp.int32, (rows, head_dim), 0) < s_len[0]
+    zero = jnp.zeros((rows, head_dim), jnp.float32)
+    dims = (((1,), (1,)), ((), ()))
+    for h in range(heads):
+        query = rotate(qkv_a[h, :, :head_dim], cos_a[...], sin_a[...])
+        key = rotate(qkv_a[h, :, head_dim:2 * head_dim], cos_a[...], sin_a[...])
+        val = qkv_a[h, :, 2 * head_dim:]
+        place = pl.ds((h // n_tp) * head_dim, head_dim)
+        keys[h % n_tp, :, place] = jnp.where(valid, key.astype(jnp.float32), zero).astype(jnp.bfloat16)
+        vals[h % n_tp, :, place] = jnp.where(valid, val.astype(jnp.float32), zero).astype(jnp.bfloat16)
+        scores = lax.dot_general(query, key, dims, preferred_element_type=jnp.float32) * scale
+        scores = jnp.where(allowed, scores, -1e30)
+        expd = jnp.exp(scores - jnp.max(scores, axis=-1, keepdims=True))
+        prob = (expd / jnp.sum(expd, axis=-1, keepdims=True)).astype(jnp.bfloat16)
+        attn_a[:, h * head_dim:(h + 1) * head_dim] = jnp.dot(prob, val, preferred_element_type=jnp.float32).astype(jnp.bfloat16)
+
+    lanes = spread.shape[1]
+    span = lanes // heads
+    one = (lax.broadcasted_iota(jnp.int32, (span, lanes), 1) // heads == lax.broadcasted_iota(jnp.int32, (span, lanes), 0))
+    spread[...] = jnp.dot(slices_b[...], jnp.where(one, 1.0, 0.0).astype(jnp.bfloat16), preferred_element_type=jnp.float32)
+    own = lax.broadcasted_iota(jnp.int32, (dec_rows, heads, lanes), 2) % heads == lax.broadcasted_iota(jnp.int32, (dec_rows, heads, lanes), 1)
+    acc[...] = jnp.zeros_like(acc)
+    inner = depth // lanes
+
+    def project(i, carry):
+        slot = lax.rem(i, FRONT_RING)
+        w_copy(i, slot).wait()
+        total = acc[...]
+        for j in range(inner):
+            part = spread[pl.ds(pl.multiple_of((i * inner + j) * dec_rows, dec_rows), dec_rows), :]
+            wide = jnp.where(own, jnp.broadcast_to(part[:, None, :], own.shape), 0.0).reshape(dec_rows * heads, lanes)
+            total = total + jnp.dot(wide.astype(jnp.bfloat16), w_buf[slot, j * lanes:(j + 1) * lanes, :], preferred_element_type=jnp.float32)
+        acc[...] = total
+
+        @pl.when(i + FRONT_RING < n_w)
+        def _():
+            w_copy(i + FRONT_RING, slot).start()
+        return carry
+    lax.fori_loop(0, n_w, project, 0)
+
+    proj = acc[...].astype(jnp.bfloat16)
+    rows_b[0] = rotate(proj[:, :head_dim], cos_b[...], sin_b[...]).astype(jnp.float32)
+    rows_b[1] = rotate(proj[:, head_dim:2 * head_dim], cos_b[...], sin_b[...]).astype(jnp.float32)
+    rows_b[2] = proj[:, 2 * head_dim:].astype(jnp.float32)
+
+    slot_of = lax.broadcasted_iota(jnp.int32, (slots_heads, head_dim), 0) // heads
+    pair = lax.broadcasted_iota(jnp.int32, (heads, slots_heads), 1)
+    same = pair % heads == lax.broadcasted_iota(jnp.int32, (heads, slots_heads), 0)
+
+    def attend(b, carry):
+        length = c_len[b]
+        mine = pl.ds(pl.multiple_of(b * heads, heads), heads)
+
+        def updated(buf, new):
+            wide = jnp.broadcast_to(new[None], (slots_heads // heads, heads, head_dim)).reshape(slots_heads, head_dim)
+            return jnp.where(slot_of == length, wide, buf[b].astype(jnp.float32)).astype(jnp.bfloat16)
+        pltpu.make_async_copy(k_cache.at[b], k_buf.at[b], k_in.at[b]).wait()
+        k_buf[b] = updated(k_buf, rows_b[1, mine])
+        pltpu.make_async_copy(v_cache.at[b], v_buf.at[b], v_in.at[b]).wait()
+        v_buf[b] = updated(v_buf, rows_b[2, mine])
+        pltpu.make_async_copy(k_buf.at[b], k_new.at[b], k_sem.at[b]).start()
+        pltpu.make_async_copy(v_buf.at[b], v_new.at[b], v_sem.at[b]).start()
+        scores = lax.dot_general(rows_b[0, mine].astype(jnp.bfloat16), k_buf[b], dims, preferred_element_type=jnp.float32) * scale
+        scores = jnp.where(same & (pair // heads <= length), scores, -1e30)
+        expd = jnp.exp(scores - jnp.max(scores, axis=-1, keepdims=True))
+        prob = (expd / jnp.sum(expd, axis=-1, keepdims=True)).astype(jnp.bfloat16)
+        attn_b[b] = jnp.dot(prob, v_buf[b], preferred_element_type=jnp.float32).astype(jnp.bfloat16)
+        return carry
+    lax.fori_loop(0, dec_rows, attend, 0)
+
+    def cache_out(b, carry):
+        pltpu.make_async_copy(k_buf.at[b], k_new.at[b], k_sem.at[b]).wait()
+        pltpu.make_async_copy(v_buf.at[b], v_new.at[b], v_sem.at[b]).wait()
+        return carry
+    lax.fori_loop(0, dec_rows, cache_out, 0)
+
+
+def rope_tables(positions, head_dim):
+    half_dim = head_dim // 2
+    inv_freq = ROPE_BASE ** (-jnp.arange(half_dim, dtype=jnp.float32) / half_dim)
+    angles = positions.astype(jnp.float32)[:, None] * inv_freq[None, :]
+    cos_tab, sin_tab = jnp.cos(angles), jnp.sin(angles)
+    return jnp.concatenate([cos_tab, cos_tab], axis=-1), jnp.concatenate([-sin_tab, sin_tab], axis=-1)
+
+
+def front_call(x_rows, y_rows, s_len, c_len, w_qkv_a, w_qkv_b, gain_a, gain_b, k_cache, v_cache, tp_size):
+    num_rows, width = x_rows.shape
+    dec_rows = y_rows.shape[0]
+    heads, wide = w_qkv_a.shape[1:]
+    head_dim = k_cache.shape[-1]
+    cache_rows = k_cache.shape[1] * heads
+    qkv_a = jnp.einsum('sd,dhe->she', rms_norm(x_rows, gain_a), w_qkv_a, preferred_element_type=jnp.float32).astype(jnp.bfloat16)
+    qkv_a = jnp.transpose(qkv_a, (1, 0, 2))
+    lanes = 256
+    span = lanes // heads
+    slices_b = jnp.transpose(rms_norm(y_rows, gain_b).reshape(dec_rows, width // span, span), (1, 0, 2)).reshape(-1, span)
+    cos_a, sin_a = rope_tables(jnp.arange(num_rows), head_dim)
+    cos_b, sin_b = (jnp.repeat(tab, heads, axis=0) for tab in rope_tables(c_len, head_dim))
+    vmem = pl.BlockSpec(memory_space=pltpu.VMEM)
+    smem = pl.BlockSpec(memory_space=pltpu.SMEM)
+    hbm = pl.BlockSpec(memory_space=pl.ANY)
+    dma = pltpu.SemaphoreType.DMA
+    depth = 2048
+    fold = heads // tp_size * head_dim
+    bf16 = jnp.bfloat16
+    cache = jax.ShapeDtypeStruct((dec_rows, cache_rows, head_dim), bf16)
+    moved = jax.ShapeDtypeStruct((tp_size, num_rows, fold), bf16)
+    return pl.pallas_call(
+        front_kernel,
+        out_shape=(jax.ShapeDtypeStruct((num_rows, heads * head_dim), bf16), moved, moved,
+                   jax.ShapeDtypeStruct((dec_rows, heads, head_dim), bf16), cache, cache),
+        in_specs=[smem] * 2 + [vmem] * 6 + [hbm] * 3,
+        out_specs=(vmem, vmem, vmem, vmem, hbm, hbm),
+        scratch_shapes=[
+            pltpu.VMEM((dec_rows, cache_rows, head_dim), bf16),
+            pltpu.VMEM((dec_rows, cache_rows, head_dim), bf16),
+            pltpu.VMEM((FRONT_RING, depth, wide), bf16),
+            pltpu.VMEM((width // span * dec_rows, lanes), jnp.float32),
+            pltpu.VMEM((dec_rows * heads, wide), jnp.float32),
+            pltpu.VMEM((3, dec_rows * heads, head_dim), jnp.float32),
+            dma((dec_rows,)), dma((dec_rows,)), dma((dec_rows,)), dma((dec_rows,)), dma((FRONT_RING,)),
+        ],
+        compiler_params=pltpu.CompilerParams(vmem_limit_bytes=40 * 1024 * 1024),
+        cost_estimate=pl.CostEstimate(flops=2 * width * heads * wide * dec_rows, bytes_accessed=60000000, transcendentals=0),
+        name='front',
+    )(s_len, c_len, qkv_a, cos_a, sin_a, slices_b, cos_b, sin_b, w_qkv_b.reshape(width * heads, wide),
+      k_cache.reshape(dec_rows, cache_rows, head_dim), v_cache.reshape(dec_rows, cache_rows, head_dim))
 
 
 def solution(mesh):
@@ -427,13 +552,16 @@
     def body(x_prompt, s_len, y_tok, k_cache, v_cache, c_len, wqkv_a, wo_a, wug_a, wd_a, norm_a, wqkv_b, wo_b, wug_b, wd_b, norm_b):
         width = x_prompt.shape[1]
         head_dim = k_cache.shape[-1]
-        attn_a, keys, vals = prefill_attention(x_prompt, s_len[0], wqkv_a[0], head_dim, norm_a[0, 0])
-        k_prompt, v_prompt = hand_off(keys, vals, tp_size, side_size)
-        attn_b, k_new, v_new = decode_attention(y_tok, c_len, k_cache[0], v_cache[0], wqkv_b[0], head_dim, norm_b[0, 0])
-        hidden, y_out = block_call(
-            x_prompt, y_tok, attn_a, attn_b, norm_a[0, 1:2].astype(jnp.float32), norm_b[0, 1:2].astype(jnp.float32),
+        dec_rows, slots, heads = k_cache.shape[1:4]
+        attn_a, keys, vals, attn_b, k_new, v_new = front_call(
+            x_prompt, y_tok, s_len, c_len, wqkv_a[0], wqkv_b[0, :, :, 0], norm_a[0, 0], norm_b[0, 0],
+            k_cache[0, :, :, :, 0], v_cache[0, :, :, :, 0], tp_size)
+        hidden, y_out, k_prompt, v_prompt = block_call(
+            x_prompt, y_tok, attn_a, attn_b.reshape(dec_rows, -1), norm_a[0, 1:2].astype(jnp.float32), norm_b[0, 1:2].astype(jnp.float32),
             wo_a[0].reshape(-1, width), jnp.transpose(wug_a[0], (1, 2, 0)), wd_a[0],
-            wo_b[0].reshape(-1, width), jnp.transpose(wug_b[0], (1, 2, 0)), wd_b[0])
-        return hidden, y_out, k_prompt, v_prompt, k_new[None], v_new[None]
+            wo_b[0].reshape(-1, width), jnp.transpose(wug_b[0], (1, 2, 0)), wd_b[0], keys, vals)
+        prompt_shape = (1, x_prompt.shape[0], heads, 1, head_dim)
+        return (hidden, y_out, k_prompt.reshape(prompt_shape), v_prompt.reshape(prompt_shape),
+                k_new.reshape(k_cache.shape), v_new.reshape(v_cache.shape))
 
     return jax.shard_map(body, mesh=mesh, in_specs=in_specs, out_specs=out_specs, check_vma=False)

time: 293 us -> 271 us (0.925)
  Pallas kernels: 198 us -> 230 us
  other arithmetic: 29.8 us -> 7.01 us
  matrix products: 36.3 us -> 16.3 us
  starting transfers between devices: 9.37 us -> 0 us
    dot_general x6 -> x1, matrix products: 36.3 us -> 16.3 us  [front_call(): jnp.einsum('sd,dhe->she', rms_norm(x_rows, gain_a), w_qkv_a, preferred_el...]
    select_n x3 -> x0, other arithmetic: 20 us -> none  [the longest x1 9.8 us: decode_attention(): val_upd = jnp.where(write_slot, val_new[:, None], v_cache)]
    pallas_call x0 -> x1, Pallas kernels: none -> 18.4 us  [front_call(): pl.pallas_call(front_kernel, out_shape=(jax.ShapeDtypeStruct((num_rows, h...]
    pallas_call x1, Pallas kernels: 198 us -> 212 us  [block_call(): pl.pallas_call(block_kernel, out_shape=(jax.ShapeDtypeStruct((rows, width...]
    unnamed x28 -> x19, local copies, waits for them, and re-layouts: 3.21 us -> 15 us
    ppermute x4 -> x0, starting transfers between devices: 9.37 us -> none  [hand_off(): moved = lax.ppermute(piece, ('tp', 'side'), pairs)]
    dynamic_update_slice x4 -> x0, local copies, waits for them, and re-layouts: 5.7 us -> none  [hand_off(): lax.dynamic_update_index_in_dim(out, moved, (tp_idx - step) % tp_size, ax...]
  transfers between devices with their start and end apart: 4 -> 0, of which waited for: 0 -> 0; matrix products, arithmetic and copies ran while one was open for 17% -> 0% of each run, Pallas kernels for 68% -> 0%
where the time goes in v2:
time: 271 us; the launch traced here: 270 us
  Pallas kernels  230 us (85%)
  matrix products  16.3 us (6%)
  local copies, waits for them, and re-layouts  15.4 us (6%)
  other arithmetic  7.01 us (3%)
    pallas_call x1, Pallas kernels, block_call(): pl.pallas_call(block_kernel, out_shape=(jax.ShapeDtypeStruct((rows, width...  212 us
    pallas_call x1, Pallas kernels, front_call(): pl.pallas_call(front_kernel, out_shape=(jax.ShapeDtypeStruct((num_rows, h...  18.4 us
    dot_general x1, matrix products, front_call(): jnp.einsum('sd,dhe->she', rms_norm(x_rows, gain_a), w_qkv_a, preferred_el...  16.3 us
    unnamed x19, local copies, waits for them, and re-layouts  15 us

profile of v2, /device:TPU:0, one launch (start us, length us, event | category | flops | bytes accessed | tf_op | source)
XLA Modules:
  0.0 270.4 jit_solution(4816948548799905219)
XLA Ops:
  1.3 0.7 convert_element_type.76
  2.0 1.0 fusion.19
  2.9 2.1 fusion.2
  5.1 0.1 fusion.23
  5.2 0.1 pad_maximum_fusion.2
  5.3 1.5 bitcast_convert_fusion
  6.7 0.9 fusion.21
  7.6 0.2 reshape.108
  7.8 0.2 copy.45
  8.0 0.5 fusion.22
  8.6 0.1 pad_maximum_fusion
  8.7 16.3 %fusion.14.qkv_a = bf16[8,256,384]{2,1,0:T(8,128)(2,1)S(1)} fusion(bf16[4096,8,384]{2,1,0:T(8,128)(2,1)} %bitcast.80, bf16[256,4096]{1,0:T(8,128)(2,1)} %x_ref.1, f32[4096]{0:T(1024)S(1)} %bitcast.79, f32[256]{0:T(256)S(1)} %add_rsqrt_fusion), kind=kOutput, calls=%fused_computation.11 | convolution fusion | flops 6447431680 | bytes 28853248 | tf_op jit(solution)/shard_map/sd,dhe->she/dot_general | solution.py:502
  25.0 2.2 copy-done
  27.2 2.2 copy-done.1
  29.4 18.4 %front.1 = (bf16[256,1024]{1,0:T(8,128)(2,1)S(1)}, bf16[4,256,256]{2,1,0:T(8,128)(2,1)S(1)}, bf16[4,256,256]{2,1,0:T(8,128)(2,1)S(1)}, bf16[8,8,128]{2,1,0:T(8,1...) custom-call(s32[1]{0:T(128)S(6)} %copy.49.s_len, s32[8]{0:T(128)S(1)} %copy-done.5, ...), custom_call_target="tpu_custom_call" | custom-call | flops 201326592 | bytes 60000000 | tf_op jit(solution)/shard_map/front/pallas_call | solution.py:518
  47.8 0.8 copy-done.2
  48.6 0.8 copy-done.3
  49.4 0.8 copy-done.4
  50.2 0.6 copy.46
  50.8 212.0 %block.1 = (bf16[256,4096]{1,0:T(8,128)(2,1)}, bf16[8,4096]{1,0:T(8,128)(2,1)}, bf16[256,1024]{1,0:T(8,128)(2,1)}, bf16[256,1024]{1,0:T(8,128)(2,1)}) custom-call(bf16[256,4096]{1,0:T(8,128)(2,1)} %x_ref.1, bf16[8,4096]{1,0:T(8,128)(2,1)} %y_ref.1, bf16[256,1024]{1,0:T(8,128)(2,1)} %copy-done.2, bf16[8,1024]{1,0:T(8,128)(2,1)} %bitcast.78, ...), custom_call_target="tpu_custom_call" | custom-call | flops 10034872320 | bytes 228065280 | tf_op jit(solution)/shard_map/block/pallas_call | solution.py:350
  262.8 2.0 copy.35
  264.7 1.9 copy.36
  266.7 3.1 %copy.50 = bf16[256,4096]{1,0:T(8,128)(2,1)} copy(bf16[256,4096]{1,0:T(8,128)(2,1)} %get-tuple-element.60) | data formatting | bytes 4194304
  269.8 0.6 copy.51
  (15 shorter events, 0.1 us)
Async XLA Ops:
  8.7 16.3 %copy-start.5 = (s32[8]{0:T(128)S(1)}, s32[8]{0:T(128)}, u32[]{:S(2)}) copy-start(s32[8]{0:T(128)} %c_len.1) | copy-start | bytes 100
  25.0 2.2 copy-start
  27.2 2.2 copy-start.1
  47.8 0.8 copy-start.2
  48.6 0.8 copy-start.3
  49.4 0.8 copy-start.4
  262.7 7.0 %copy-start.6 = (bf16[8,4096]{1,0:T(8,128)(2,1)S(1)}, bf16[8,4096]{1,0:T(8,128)(2,1)}, u32[]{:S(2)}) copy-start(bf16[8,4096]{1,0:T(8,128)(2,1)} %get-tuple-element.61) | copy-start | bytes 196612

commit v3 on v2

--- a/solution.py
+++ b/solution.py
@@ -32,8 +32,10 @@
 HALF_ROWS = 128
 RING = 3
 WIRE = 128
+WIRE_ROWS = 128
 FRONT_RING = 4
-SKEW = 2
+SKEW = 3
+RATE = 1
 
 
 def block_kernel(x_ref, y_ref, attn_a_ref, attn_b_ref, norm_a_ref, norm_b_ref, wo_a, wug_a, wd_a, wo_b, wug_b, wd_b, keys, vals,
@@ -42,7 +44,8 @@
                  rs_send, rs_recv, ag_send, ag_recv, rsd_send, rsd_recv, agd_send, agd_recv, ug_sem, dn_sem, out_sem, hand_send, hand_recv):
     ffn, width = wd_a.shape
     mid = width // 2
-    per = mid // WIRE
+    cuts = HALF_ROWS // WIRE_ROWS
+    per = mid // WIRE * cuts
     n_up = -(-ffn // COLS)
     last_up = ffn - COLS
     n_dn = width // 512
@@ -73,10 +76,13 @@
     def agd_copy(ar, half):
         return remote(hid_d.at[ar, half], hid_d.at[ar, half], agd_send.at[ar, half], agd_recv.at[ar, half], bwd(half))
 
+    def place(half, g):
+        row = (lax.rem(g // per, 2) * cuts + lax.rem(g, cuts)) * WIRE_ROWS
+        col = half * mid + lax.rem(g, per) // cuts * WIRE
+        return pl.ds(pl.multiple_of(row, WIRE_ROWS), WIRE_ROWS), pl.ds(pl.multiple_of(col, WIRE), WIRE)
+
     def out_copy(half, g):
-        row = (g // per - 2) * HALF_ROWS
-        col = pl.multiple_of(half * mid + lax.rem(g, per) * WIRE, WIRE)
-        return pltpu.make_async_copy(hid.at[half, g], out_a.at[pl.ds(pl.multiple_of(row, HALF_ROWS), HALF_ROWS), pl.ds(col, WIRE)], out_sem.at[half])
+        return pltpu.make_async_copy(hid.at[half, g], out_a.at[place(half, g)], out_sem.at[half])
 
     def ug_copy(src, i, slot):
         row = pl.multiple_of(jnp.minimum(i * COLS, last_up), 64)
@@ -88,6 +94,14 @@
 
     def slot_step(s, first, last, second, dec_at):
         ar = 1 if second else 0
+        if not second:
+            for which in range(2):
+                turn = s - hand_at - 8 * which
+
+                @pl.when((turn >= 0) & (turn < 8) & (lax.rem(turn, 2) == 0))
+                def _():
+                    hand_copy(which, turn // 2).start()
+
         for half in range(2):
             where_at = pos(half)
             g = first + s - SKEW * where_at
@@ -111,9 +125,7 @@
                 if second:
                     base = hid[half, g - 2 * per]
                 else:
-                    row = pl.multiple_of((g // per) * HALF_ROWS, HALF_ROWS)
-                    col = pl.multiple_of(half * mid + lax.rem(g, per) * WIRE, WIRE)
-                    base = x_ref[pl.ds(row, HALF_ROWS), pl.ds(col, WIRE)]
+                    base = x_ref[place(half, g)]
                 hid[half, g] = (base.astype(jnp.float32) + total).astype(jnp.bfloat16)
                 ag_copy(half, g).start()
                 if second:
@@ -206,7 +218,8 @@
     def put_part(j, first, total):
         half = lax.rem(j, 2)
         for q in range(512 // WIRE):
-            part[half, first + (j // 2) * (512 // WIRE) + q] = total[:, q * WIRE:(q + 1) * WIRE]
+            for r in range(cuts):
+                part[half, first + ((j // 2) * (512 // WIRE) + q) * cuts + r] = total[r * WIRE_ROWS:(r + 1) * WIRE_ROWS, q * WIRE:(q + 1) * WIRE]
 
     def put_dec(ar, j, total):
         half = lax.rem(j, 2)
@@ -216,19 +229,22 @@
         pass
 
     def norm_rows(first):
-        def square(q, acc):
-            val = hid[q // per, first + lax.rem(q, per)].astype(jnp.float32)
-            val = val * val
-            return acc + val
-        acc = lax.fori_loop(0, 2 * per, square, jnp.zeros((HALF_ROWS, WIRE), jnp.float32))
-        inv = lax.rsqrt(jnp.sum(acc, axis=-1, keepdims=True) / width + NORM_EPS)
-
-        def scale(q, carry):
-            cols = pl.ds(pl.multiple_of(q * WIRE, WIRE), WIRE)
-            val = hid[q // per, first + lax.rem(q, per)].astype(jnp.float32)
-            normed[:, cols] = (val * inv * norm_a_ref[:, cols]).astype(jnp.bfloat16)
-            return carry
-        lax.fori_loop(0, 2 * per, scale, 0)
+        blocks = per // cuts
+        for r in range(cuts):
+            def load(q, r=r):
+                return hid[q // blocks, first + lax.rem(q, blocks) * cuts + r].astype(jnp.float32)
+
+            def square(q, acc, load=load):
+                val = load(q)
+                return acc + val * val
+            acc = lax.fori_loop(0, 2 * blocks, square, jnp.zeros((WIRE_ROWS, WIRE), jnp.float32))
+            inv = lax.rsqrt(jnp.sum(acc, axis=-1, keepdims=True) / width + NORM_EPS)
+
+            def scale(q, carry, load=load, inv=inv, r=r):
+                cols = pl.ds(pl.multiple_of(q * WIRE, WIRE), WIRE)
+                normed[r * WIRE_ROWS:(r + 1) * WIRE_ROWS, cols] = (load(q) * inv * norm_a_ref[:, cols].astype(jnp.float32)).astype(jnp.bfloat16)
+                return carry
+            lax.fori_loop(0, 2 * blocks, scale, 0)
 
     side = lax.axis_index('side')
     n_side = lax.axis_size('side')
@@ -252,27 +268,17 @@
             pl.semaphore_signal(barrier, inc=1, device_id={'tp': lax.rem(z + 4 + step, 4)}, device_id_type=MESH_ID)
 
     for slot in range(RING):
-        dn_copy(wo_b, slot, slot).start()
+        dn_copy(wo_a, slot, slot).start()
     for slot in range(RING):
         ug_copy(wug_a, slot, slot).start()
 
     pl.semaphore_wait(barrier, jnp.where((z == 0) | (z == 3), 5, 6))
-    for step in range(4):
-        hand_copy(0, step).start()
-
-    def dec_proj(j, slot):
-        put_dec(0, j, jnp.dot(attn_b_ref[...], dn_buf[slot, :attn_b_ref.shape[1], :], preferred_element_type=jnp.float32))
-    dn_phase(wo_b, wo_a, 0, dec_proj, no_comm)
-
-    def prompt_proj(j, slot):
-        total = jnp.dot(attn_a_ref[...], dn_buf[slot, :attn_a_ref.shape[1], :], preferred_element_type=jnp.float32)
-        put_part(j, 0, total[:HALF_ROWS])
-        put_part(j, per, total[HALF_ROWS:])
-    dn_phase(wo_a, wd_a, n_dn, prompt_proj, no_comm)
 
     depth = 6 * SKEW
-    flow_one = (0, 2 * per, False, 0)
-    dec_two = per + n_up + n_dn
+    dec_one = per
+    dec_two = per + RATE * (n_up + n_dn)
+    hand_at = per + depth + 1
+    flow_one = (0, 2 * per, False, dec_one)
     flow_c0 = (2 * per, 3 * per, True, dec_two)
     flow_c1 = (2 * per, 4 * per, True, dec_two)
 
@@ -282,31 +288,41 @@
             return carry
         lax.fori_loop(first, last, at, 0)
 
-    def beside(first, count, flow):
+    def beside(first, last, flow, rate):
         def at(i):
-            @pl.when(i < count)
-            def _():
-                slot_step(first + i, *flow)
+            def one(s, carry):
+                slot_step(s, *flow)
+                return carry
+            lax.fori_loop(jnp.minimum(first + i * rate, last), jnp.minimum(first + (i + 1) * rate, last), one, 0)
         return at
 
-    slots(0, per + depth, flow_one)
-    for step in range(4):
-        hand_copy(1, step).start()
+    def prompt_proj(j, slot):
+        total = jnp.dot(attn_a_ref[...], dn_buf[slot, :attn_a_ref.shape[1], :], preferred_element_type=jnp.float32)
+        put_part(j, 0, total[:HALF_ROWS])
+        put_part(j, per, total[HALF_ROWS:])
+    dn_phase(wo_a, wo_b, 0, prompt_proj, no_comm)
+
+    def dec_proj(j, slot):
+        put_dec(0, j, jnp.dot(attn_b_ref[...], dn_buf[slot, :attn_b_ref.shape[1], :], preferred_element_type=jnp.float32))
+    dn_phase(wo_b, wd_a, n_dn, dec_proj, beside(0, n_dn, flow_one, 1))
+    slots(n_dn, per + depth, flow_one)
 
     norm_rows(0)
-    lead = min(n_up, per)
-    up_phase(wug_a, wug_a, 0, normed, act, beside(per + depth, lead, flow_one))
-    dn_phase(wd_a, wd_a, 2 * n_dn, lambda j, slot: put_part(j, 2 * per, down_dot(act, slot)), beside(per + depth + lead, per - lead, flow_one))
+    ready, drained = per + depth, 2 * per + depth
+    lead = min(RATE * n_up, drained - ready)
+    up_phase(wug_a, wug_a, 0, normed, act, beside(ready, ready + lead, flow_one, RATE))
+    dn_phase(wd_a, wd_a, 2 * n_dn, lambda j, slot: put_part(j, 2 * per, down_dot(act, slot)), beside(ready + lead, drained, flow_one, -(-(drained - ready - lead) // n_dn)))
 
     norm_rows(per)
-    up_phase(wug_a, wug_b, n_up, normed, act, beside(0, lead, flow_c0))
-    dn_phase(wd_a, wd_b, 3 * n_dn, lambda j, slot: put_part(j, 3 * per, down_dot(act, slot)), beside(lead, per - lead, flow_c0))
+    lead = min(RATE * n_up, per)
+    up_phase(wug_a, wug_b, n_up, normed, act, beside(0, lead, flow_c0, RATE))
+    dn_phase(wd_a, wd_b, 3 * n_dn, lambda j, slot: put_part(j, 3 * per, down_dot(act, slot)), beside(lead, per, flow_c0, -(-(per - lead) // n_dn)))
 
     val = jnp.concatenate([hid_d[0, 0], hid_d[0, 1]], axis=-1).astype(jnp.float32)
     inv = lax.rsqrt(jnp.mean(val * val, axis=-1, keepdims=True) + NORM_EPS)
-    normed_d[...] = (val * inv * norm_b_ref[...]).astype(jnp.bfloat16)
-    up_phase(wug_b, None, 2 * n_up, normed_d, act_d, beside(per, n_up, flow_c1))
-    dn_phase(wd_b, None, 4 * n_dn, lambda j, slot: put_dec(1, j, down_dot(act_d, slot)), beside(per + n_up, n_dn, flow_c1))
+    normed_d[...] = (val * inv * norm_b_ref[...].astype(jnp.float32)).astype(jnp.bfloat16)
+    up_phase(wug_b, None, 2 * n_up, normed_d, act_d, beside(per, per + RATE * n_up, flow_c1, RATE))
+    dn_phase(wd_b, None, 4 * n_dn, lambda j, slot: put_dec(1, j, down_dot(act_d, slot)), beside(per + RATE * n_up, dec_two, flow_c1, RATE))
     slots(dec_two, max(2 * per, dec_two + 1) + depth, flow_c1)
 
     for which in range(2):
@@ -341,7 +357,8 @@
     dec_rows = y_rows.shape[0]
     ffn = wd_a.shape[0]
     mid = width // 2
-    per = mid // WIRE
+    cuts = HALF_ROWS // WIRE_ROWS
+    per = mid // WIRE * cuts
     n_up = -(-ffn // COLS)
     vmem = pl.BlockSpec(memory_space=pltpu.VMEM)
     hbm = pl.BlockSpec(memory_space=pl.ANY)
@@ -354,9 +371,9 @@
         in_specs=[vmem] * 6 + [hbm] * 8,
         out_specs=(hbm, vmem, hbm, hbm),
         scratch_shapes=[
-            pltpu.VMEM((2, 4 * per, HALF_ROWS, WIRE), jnp.float32),
-            pltpu.VMEM((2, 4 * per, HALF_ROWS, WIRE), jnp.float32),
-            pltpu.VMEM((2, 4 * per, HALF_ROWS, WIRE), jnp.bfloat16),
+            pltpu.VMEM((2, 4 * per, WIRE_ROWS, WIRE), jnp.float32),
+            pltpu.VMEM((2, 4 * per, WIRE_ROWS, WIRE), jnp.float32),
+            pltpu.VMEM((2, 4 * per, WIRE_ROWS, WIRE), jnp.bfloat16),
             pltpu.VMEM((2, 2, dec_rows, mid), jnp.float32),
             pltpu.VMEM((2, 2, dec_rows, mid), jnp.float32),
             pltpu.VMEM((2, 2, dec_rows, mid), jnp.bfloat16),
@@ -530,7 +547,7 @@
             pltpu.VMEM((3, dec_rows * heads, head_dim), jnp.float32),
             dma((dec_rows,)), dma((dec_rows,)), dma((dec_rows,)), dma((dec_rows,)), dma((FRONT_RING,)),
         ],
-        compiler_params=pltpu.CompilerParams(vmem_limit_bytes=40 * 1024 * 1024),
+        compiler_params=pltpu.CompilerParams(vmem_limit_bytes=62 * 1024 * 1024),
         cost_estimate=pl.CostEstimate(flops=2 * width * heads * wide * dec_rows, bytes_accessed=60000000, transcendentals=0),
         name='front',
     )(s_len, c_len, qkv_a, cos_a, sin_a, slices_b, cos_b, sin_b, w_qkv_b.reshape(width * heads, wide),
@@ -557,7 +574,7 @@
             x_prompt, y_tok, s_len, c_len, wqkv_a[0], wqkv_b[0, :, :, 0], norm_a[0, 0], norm_b[0, 0],
             k_cache[0, :, :, :, 0], v_cache[0, :, :, :, 0], tp_size)
         hidden, y_out, k_prompt, v_prompt = block_call(
-            x_prompt, y_tok, attn_a, attn_b.reshape(dec_rows, -1), norm_a[0, 1:2].astype(jnp.float32), norm_b[0, 1:2].astype(jnp.float32),
+            x_prompt, y_tok, attn_a, attn_b.reshape(dec_rows, -1), norm_a[0, 1:2], norm_b[0, 1:2],
             wo_a[0].reshape(-1, width), jnp.transpose(wug_a[0], (1, 2, 0)), wd_a[0],
             wo_b[0].reshape(-1, width), jnp.transpose(wug_b[0], (1, 2, 0)), wd_b[0], keys, vals)
         prompt_shape = (1, x_prompt.shape[0], heads, 1, head_dim)

time: 271 us -> 268 us (0.989)
  local copies, waits for them, and re-layouts: 15.4 us -> 11.3 us
    unnamed x19 -> x9, local copies, waits for them, and re-layouts: 15 us -> 9 us
    pallas_call x1, Pallas kernels: 18.4 us -> 21.2 us  [front_call(): pl.pallas_call(front_kernel, out_shape=(jax.ShapeDtypeStruct((num_rows, h...]
where the time goes in v3:
time: 268 us
  Pallas kernels  232 us (87%)
  matrix products  15.1 us (6%)
  local copies, waits for them, and re-layouts  11.3 us (4%)
  other arithmetic  7.69 us (3%)
    pallas_call x1, Pallas kernels, block_call(): pl.pallas_call(block_kernel, out_shape=(jax.ShapeDtypeStruct((rows, width...  211 us
    pallas_call x1, Pallas kernels, front_call(): pl.pallas_call(front_kernel, out_shape=(jax.ShapeDtypeStruct((num_rows, h...  21.2 us
    dot_general x1, matrix products, front_call(): jnp.einsum('sd,dhe->she', rms_norm(x_rows, gain_a), w_qkv_a, preferred_el...  15.1 us
    unnamed x9, local copies, waits for them, and re-layouts  9 us

profile of v3, /device:TPU:0, one launch (start us, length us, event | category | flops | bytes accessed | tf_op | source)
XLA Modules:
  0.0 267.8 jit_solution(9653135895704382648)
XLA Ops:
  0.6 0.0 copy-start
  1.5 0.7 convert_element_type.66
  2.1 1.0 fusion.19
  3.1 2.1 fusion.2
  5.2 0.1 fusion.23
  5.3 0.1 pad_maximum_fusion.2
  5.4 0.6 broadcast_bitcast_fusion.1.cos_b
  6.0 0.6 broadcast_bitcast_fusion.sin_b
  6.6 1.5 slice_bitcast_fusion
  8.1 0.9 fusion.21
  9.0 0.2 reshape.80
  9.2 0.9 copy.45
  10.1 0.5 fusion.22
  10.6 0.8 pad_maximum_fusion
  11.4 0.0 copy-done
  11.4 15.1 %fusion.14.qkv_a = bf16[8,256,384]{2,1,0:T(8,128)(2,1)} fusion(bf16[4096,8,384]{2,1,0:T(8,128)(2,1)} %bitcast.78, bf16[256,4096]{1,0:T(8,128)(2,1)S(1)} %copy-done, f32[4096]{0:T(1024)S(1)} %bitcast.77, f32[256]{0:T(256)S(1)} %add_rsqrt_fusion), kind=kOutput, calls=%fused_computation.11 | convolution fusion | flops 6447431680 | bytes 28853248 | tf_op jit(solution)/shard_map/sd,dhe->she/dot_general | solution.py:519
  26.5 21.2 %front.1 = (bf16[256,1024]{1,0:T(8,128)(2,1)}, bf16[4,256,256]{2,1,0:T(8,128)(2,1)}, bf16[4,256,256]{2,1,0:T(8,128)(2,1)}, bf16[8,8,128]{2,1,0:T(8,128)(2,1)}, b...) custom-call(s32[1]{0:T(128)S(6)} %copy.49.s_len, s32[8]{0:T(128)} %c_len.1, ...), custom_call_target="tpu_custom_call" | custom-call | flops 201326592 | bytes 60000000 | tf_op jit(solution)/shard_map/front/pallas_call | solution.py:535
  47.7 1.3 copy.46
  49.0 211.1 %block.1 = (bf16[256,4096]{1,0:T(8,128)(2,1)}, bf16[8,4096]{1,0:T(8,128)(2,1)}, bf16[256,1024]{1,0:T(8,128)(2,1)}, bf16[256,1024]{1,0:T(8,128)(2,1)}) custom-call(bf16[256,4096]{1,0:T(8,128)(2,1)} %x_ref.1, bf16[8,4096]{1,0:T(8,128)(2,1)} %y_ref.1, bf16[256,1024]{1,0:T(8,128)(2,1)} %get-tuple-element.16.attn_a_ref, bf16[8,1024]{1,0:T(8,128)(2,1)} %bitcast.75, ...), custom_call_target="tpu_custom_call" | custom-call | flops 10034872320 | bytes 228065280 | tf_op jit(solution)/shard_map/block/pallas_call | solution.py:367
  260.1 0.0 copy-start.1
  260.2 2.0 copy.35
  262.1 1.9 copy.36
  264.1 3.1 %copy.50 = bf16[256,4096]{1,0:T(8,128)(2,1)} copy(bf16[256,4096]{1,0:T(8,128)(2,1)} %get-tuple-element.60) | data formatting | bytes 4194304
  267.2 0.6 copy.51
  (5 shorter events, 0.0 us)
Async XLA Ops:
  0.6 10.8 %copy-start = (bf16[256,4096]{1,0:T(8,128)(2,1)S(1)}, bf16[256,4096]{1,0:T(8,128)(2,1)}, u32[]{:S(2)}) copy-start(bf16[256,4096]{1,0:T(8,128)(2,1)} %x_ref.1) | copy-start | bytes 6291460
  260.1 7.0 %copy-start.1 = (bf16[8,4096]{1,0:T(8,128)(2,1)S(1)}, bf16[8,4096]{1,0:T(8,128)(2,1)}, u32[]{:S(2)}) copy-start(bf16[8,4096]{1,0:T(8,128)(2,1)} %get-tuple-element.61) | copy-start | bytes 196612

commit v4 on v3

--- a/solution.py
+++ b/solution.py
@@ -33,15 +33,15 @@
 RING = 3
 WIRE = 128
 WIRE_ROWS = 128
-FRONT_RING = 4
 SKEW = 3
 RATE = 1
 
 
-def block_kernel(x_ref, y_ref, attn_a_ref, attn_b_ref, norm_a_ref, norm_b_ref, wo_a, wug_a, wd_a, wo_b, wug_b, wd_b, keys, vals,
-                 out_a, out_b, k_out, v_out,
+def block_kernel(c_len, x_ref, y_ref, attn_a_ref, slices_b, cos_b, sin_b, norm_a_ref, norm_b_ref, wo_a, wug_a, wd_a, wo_b, wug_b, wd_b, keys, vals, wqkv_b, k_cache, v_cache,
+                 out_a, out_b, k_out, v_out, fresh,
                  part, rcv, hid, part_d, rcv_d, hid_d, normed, act, normed_d, act_d, ug_buf, dn_buf,
-                 rs_send, rs_recv, ag_send, ag_recv, rsd_send, rsd_recv, agd_send, agd_recv, ug_sem, dn_sem, out_sem, hand_send, hand_recv):
+                 rs_send, rs_recv, ag_send, ag_recv, rsd_send, rsd_recv, agd_send, agd_recv, ug_sem, dn_sem, out_sem, hand_send, hand_recv,
+                 k_buf, v_buf, w_buf, spread, acc, rows_b, attn_rows, k_in, v_in, w_sem):
     ffn, width = wd_a.shape
     mid = width // 2
     cuts = HALF_ROWS // WIRE_ROWS
@@ -269,13 +269,32 @@
 
     for slot in range(RING):
         dn_copy(wo_a, slot, slot).start()
+    heads = wqkv_b.shape[0] // width
+    head_dim = cos_b.shape[1]
+    dec_rows, slots_heads, _ = k_cache.shape
+    w_depth = w_buf.shape[1]
+    n_w = wqkv_b.shape[0] // w_depth
+
+    def w_copy(i, slot):
+        return pltpu.make_async_copy(wqkv_b.at[pl.ds(pl.multiple_of(i * w_depth, w_depth), w_depth), :], w_buf.at[slot], w_sem.at[slot])
+
+    def cache_copies(b):
+        slot = lax.rem(b, 2)
+        return (pltpu.make_async_copy(k_cache.at[b], k_buf.at[slot], k_in.at[slot]),
+                pltpu.make_async_copy(v_cache.at[b], v_buf.at[slot], v_in.at[slot]))
+
+    for slot in range(RING):
+        w_copy(slot, slot).start()
+    for b in range(2):
+        for copy in cache_copies(b):
+            copy.start()
     for slot in range(RING):
         ug_copy(wug_a, slot, slot).start()
 
     pl.semaphore_wait(barrier, jnp.where((z == 0) | (z == 3), 5, 6))
 
     depth = 6 * SKEW
-    dec_one = per
+    dec_one = 2 * per
     dec_two = per + RATE * (n_up + n_dn)
     hand_at = per + depth + 1
     flow_one = (0, 2 * per, False, dec_one)
@@ -302,13 +321,83 @@
         put_part(j, per, total[HALF_ROWS:])
     dn_phase(wo_a, wo_b, 0, prompt_proj, no_comm)
 
+    lanes = spread.shape[1]
+    span = lanes // heads
+    one = (lax.broadcasted_iota(jnp.int32, (span, lanes), 1) // heads == lax.broadcasted_iota(jnp.int32, (span, lanes), 0))
+    spread[...] = jnp.dot(slices_b[...], jnp.where(one, 1.0, 0.0).astype(jnp.bfloat16), preferred_element_type=jnp.float32)
+    acc[...] = jnp.zeros_like(acc)
+    inner = w_depth // lanes
+    early = beside(0, n_w, flow_one, 1)
+
+    def project(i, carry):
+        own = lax.broadcasted_iota(jnp.int32, (dec_rows, heads, lanes), 2) % heads == lax.broadcasted_iota(jnp.int32, (dec_rows, heads, lanes), 1)
+        slot = lax.rem(i, RING)
+        w_copy(i, slot).wait()
+        total = acc[...]
+        for j in range(inner):
+            piece = spread[pl.ds(pl.multiple_of((i * inner + j) * dec_rows, dec_rows), dec_rows), :]
+            wide = jnp.where(own, jnp.broadcast_to(piece[:, None, :], own.shape), 0.0).reshape(dec_rows * heads, lanes)
+            total = total + jnp.dot(wide.astype(jnp.bfloat16), w_buf[slot, j * lanes:(j + 1) * lanes, :], preferred_element_type=jnp.float32)
+        acc[...] = total
+
+        @pl.when(i + RING < n_w)
+        def _():
+            w_copy(i + RING, slot).start()
+        early(i)
+        return carry
+    lax.fori_loop(0, n_w, project, 0)
+
+    def rotate(val):
+        val = val.astype(jnp.float32)
+        swapped = jnp.concatenate([val[:, head_dim // 2:], val[:, :head_dim // 2]], axis=-1)
+        return (val * cos_b[...] + swapped * sin_b[...]).astype(jnp.bfloat16).astype(jnp.float32)
+
+    proj = acc[...].astype(jnp.bfloat16)
+    rows_b[0] = rotate(proj[:, :head_dim])
+    rows_b[1] = rotate(proj[:, head_dim:2 * head_dim])
+    rows_b[2] = proj[:, 2 * head_dim:].astype(jnp.float32)
+    fresh[0] = rows_b[1]
+    fresh[1] = rows_b[2]
+
+    late = beside(n_w, n_w + dec_rows, flow_one, 1)
+
+    def attend(b, carry):
+        length = c_len[b]
+        slot = lax.rem(b, 2)
+        mine = pl.ds(pl.multiple_of(b * heads, heads), heads)
+        slot_of = lax.broadcasted_iota(jnp.int32, (slots_heads, head_dim), 0) // heads
+        pair = lax.broadcasted_iota(jnp.int32, (heads, slots_heads), 1)
+        same = pair % heads == lax.broadcasted_iota(jnp.int32, (heads, slots_heads), 0)
+
+        def updated(buf, new):
+            wide = jnp.broadcast_to(new[None], (slots_heads // heads, heads, head_dim)).reshape(slots_heads, head_dim)
+            return jnp.where(slot_of == length, wide, buf[slot].astype(jnp.float32)).astype(jnp.bfloat16)
+        for copy in cache_copies(b):
+            copy.wait()
+        scores = lax.dot_general(rows_b[0, mine].astype(jnp.bfloat16), updated(k_buf, rows_b[1, mine]), (((1,), (1,)), ((), ())), preferred_element_type=jnp.float32) * head_dim ** -0.5
+        scores = jnp.where(same & (pair // heads <= length), scores, -1e30)
+        expd = jnp.exp(scores - jnp.max(scores, axis=-1, keepdims=True))
+        prob = (expd / jnp.sum(expd, axis=-1, keepdims=True)).astype(jnp.bfloat16)
+        attn_rows[b] = jnp.dot(prob, updated(v_buf, rows_b[2, mine]), preferred_element_type=jnp.float32)
+
+        @pl.when(b + 2 < dec_rows)
+        def _():
+            for copy in cache_copies(b + 2):
+                copy.start()
+        late(b)
+        return carry
+    lax.fori_loop(0, dec_rows, attend, 0)
+
+    attn_b = jnp.concatenate([attn_rows[:, h, :] for h in range(heads)], axis=-1).astype(jnp.bfloat16)
+
     def dec_proj(j, slot):
-        put_dec(0, j, jnp.dot(attn_b_ref[...], dn_buf[slot, :attn_b_ref.shape[1], :], preferred_element_type=jnp.float32))
-    dn_phase(wo_b, wd_a, n_dn, dec_proj, beside(0, n_dn, flow_one, 1))
-    slots(n_dn, per + depth, flow_one)
+        put_dec(0, j, jnp.dot(attn_b, dn_buf[slot, :heads * head_dim, :], preferred_element_type=jnp.float32))
+    first = n_w + dec_rows
+    dn_phase(wo_b, wd_a, n_dn, dec_proj, beside(first, min(first + n_dn, dec_one), flow_one, 1))
+    slots(min(first + n_dn, dec_one), per + depth, flow_one)
 
     norm_rows(0)
-    ready, drained = per + depth, 2 * per + depth
+    ready, drained = per + depth, max(2 * per, dec_one + 1) + depth
     lead = min(RATE * n_up, drained - ready)
     up_phase(wug_a, wug_a, 0, normed, act, beside(ready, ready + lead, flow_one, RATE))
     dn_phase(wd_a, wd_a, 2 * n_dn, lambda j, slot: put_part(j, 2 * per, down_dot(act, slot)), beside(ready + lead, drained, flow_one, -(-(drained - ready - lead) // n_dn)))
@@ -352,7 +441,7 @@
         pltpu.make_async_copy(hid.at[half, pl.ds(0, 2 * per)], hid.at[half, pl.ds(2 * per, 2 * per)], out_sem.at[half]).wait()
 
 
-def block_call(x_rows, y_rows, attn_a, attn_b, norm_a, norm_b, wo_a, wug_a, wd_a, wo_b, wug_b, wd_b, keys, vals):
+def block_call(c_len, x_rows, y_rows, attn_a, slices_b, cos_b, sin_b, norm_a, norm_b, wo_a, wug_a, wd_a, wo_b, wug_b, wd_b, keys, vals, wqkv_b, k_cache, v_cache):
     rows, width = x_rows.shape
     dec_rows = y_rows.shape[0]
     ffn = wd_a.shape[0]
@@ -367,9 +456,10 @@
     return pl.pallas_call(
         block_kernel,
         out_shape=(jax.ShapeDtypeStruct((rows, width), jnp.bfloat16), jax.ShapeDtypeStruct((dec_rows, width), jnp.bfloat16),
-                   *[jax.ShapeDtypeStruct((rows, keys.shape[0] * keys.shape[2]), jnp.bfloat16)] * 2),
-        in_specs=[vmem] * 6 + [hbm] * 8,
-        out_specs=(hbm, vmem, hbm, hbm),
+                   *[jax.ShapeDtypeStruct((rows, keys.shape[0] * keys.shape[2]), jnp.bfloat16)] * 2,
+                   jax.ShapeDtypeStruct((2,) + cos_b.shape, jnp.float32)),
+        in_specs=[pl.BlockSpec(memory_space=pltpu.SMEM)] + [vmem] * 8 + [hbm] * 11,
+        out_specs=(hbm, vmem, hbm, hbm, vmem),
         scratch_shapes=[
             pltpu.VMEM((2, 4 * per, WIRE_ROWS, WIRE), jnp.float32),
             pltpu.VMEM((2, 4 * per, WIRE_ROWS, WIRE), jnp.float32),
@@ -386,36 +476,38 @@
             dma((2,)), dma((2, 4 * per)), dma((2,)), dma((2, 4 * per)),
             dma((2, 2)), dma((2, 2)), dma((2, 2)), dma((2, 2)),
             dma((RING,)), dma((RING,)), dma((2,)), dma((2, 4)), dma((2, 4)),
+            pltpu.VMEM((2,) + k_cache.shape[1:], jnp.bfloat16),
+            pltpu.VMEM((2,) + k_cache.shape[1:], jnp.bfloat16),
+            pltpu.VMEM((RING, 2048, wqkv_b.shape[1]), jnp.bfloat16),
+            pltpu.VMEM((slices_b.shape[0], 256), jnp.float32),
+            pltpu.VMEM((cos_b.shape[0], wqkv_b.shape[1]), jnp.float32),
+            pltpu.VMEM((3,) + cos_b.shape, jnp.float32),
+            pltpu.VMEM((dec_rows, cos_b.shape[0] // dec_rows, cos_b.shape[1]), jnp.float32),
+            dma((2,)), dma((2,)), dma((RING,)),
         ],
         compiler_params=pltpu.CompilerParams(collective_id=0, has_side_effects=True, vmem_limit_bytes=62 * 1024 * 1024),
         cost_estimate=pl.CostEstimate(flops=weights * (rows + dec_rows) // 2, bytes_accessed=weights * 3, transcendentals=0),
         name='block',
-    )(x_rows, y_rows, attn_a, attn_b, norm_a, norm_b, wo_a, wug_a, wd_a, wo_b, wug_b, wd_b, keys, vals)
-
-
-def front_kernel(s_len, c_len, qkv_a, cos_a, sin_a, slices_b, cos_b, sin_b, wqkv_b, k_cache, v_cache,
-                 attn_a, keys, vals, attn_b, k_new, v_new,
-                 k_buf, v_buf, w_buf, spread, acc, rows_b, k_in, v_in, k_sem, v_sem, w_sem):
+    )(c_len, x_rows, y_rows, attn_a, slices_b, cos_b, sin_b, norm_a, norm_b, wo_a, wug_a, wd_a, wo_b, wug_b, wd_b, keys, vals, wqkv_b, k_cache, v_cache)
+
+
+def front_kernel(s_len, qkv_a, cos_a, sin_a, k_cache, v_cache, attn_a, keys, vals, k_new, v_new, k_buf, v_buf, k_in, v_in, k_sem, v_sem):
     heads, rows, _ = qkv_a.shape
     head_dim = cos_a.shape[1]
     half = head_dim // 2
-    dec_rows, slots_heads, _ = k_cache.shape
+    dec_rows = k_cache.shape[0]
     n_tp = keys.shape[0]
-    depth = w_buf.shape[1]
-    n_w = wqkv_b.shape[0] // depth
     scale = head_dim ** -0.5
 
-    def w_copy(i, slot):
-        return pltpu.make_async_copy(wqkv_b.at[pl.ds(pl.multiple_of(i * depth, depth), depth), :], w_buf.at[slot], w_sem.at[slot])
-
-    for slot in range(FRONT_RING):
-        w_copy(slot, slot).start()
-
-    def cache_in(b, carry):
-        pltpu.make_async_copy(k_cache.at[b], k_buf.at[b], k_in.at[b]).start()
-        pltpu.make_async_copy(v_cache.at[b], v_buf.at[b], v_in.at[b]).start()
-        return carry
-    lax.fori_loop(0, dec_rows, cache_in, 0)
+    def cache_in(b):
+        return (pltpu.make_async_copy(k_cache.at[b], k_buf.at[b], k_in.at[b]), pltpu.make_async_copy(v_cache.at[b], v_buf.at[b], v_in.at[b]))
+
+    def cache_out(b):
+        return (pltpu.make_async_copy(k_buf.at[b], k_new.at[b], k_sem.at[b]), pltpu.make_async_copy(v_buf.at[b], v_new.at[b], v_sem.at[b]))
+
+    for b in range(dec_rows):
+        for copy in cache_in(b):
+            copy.start()
 
     def rotate(val, cos_tab, sin_tab):
         val = val.astype(jnp.float32)
@@ -440,66 +532,49 @@
         expd = jnp.exp(scores - jnp.max(scores, axis=-1, keepdims=True))
         prob = (expd / jnp.sum(expd, axis=-1, keepdims=True)).astype(jnp.bfloat16)
         attn_a[:, h * head_dim:(h + 1) * head_dim] = jnp.dot(prob, val, preferred_element_type=jnp.float32).astype(jnp.bfloat16)
-
-    lanes = spread.shape[1]
-    span = lanes // heads
-    one = (lax.broadcasted_iota(jnp.int32, (span, lanes), 1) // heads == lax.broadcasted_iota(jnp.int32, (span, lanes), 0))
-    spread[...] = jnp.dot(slices_b[...], jnp.where(one, 1.0, 0.0).astype(jnp.bfloat16), preferred_element_type=jnp.float32)
-    own = lax.broadcasted_iota(jnp.int32, (dec_rows, heads, lanes), 2) % heads == lax.broadcasted_iota(jnp.int32, (dec_rows, heads, lanes), 1)
-    acc[...] = jnp.zeros_like(acc)
-    inner = depth // lanes
-
-    def project(i, carry):
-        slot = lax.rem(i, FRONT_RING)
-        w_copy(i, slot).wait()
-        total = acc[...]
-        for j in range(inner):
-            part = spread[pl.ds(pl.multiple_of((i * inner + j) * dec_rows, dec_rows), dec_rows), :]
-            wide = jnp.where(own, jnp.broadcast_to(part[:, None, :], own.shape), 0.0).reshape(dec_rows * heads, lanes)
-            total = total + jnp.dot(wide.astype(jnp.bfloat16), w_buf[slot, j * lanes:(j + 1) * lanes, :], preferred_element_type=jnp.float32)
-        acc[...] = total
-
-        @pl.when(i + FRONT_RING < n_w)
-        def _():
-            w_copy(i + FRONT_RING, slot).start()
-        return carry
-    lax.fori_loop(0, n_w, project, 0)
-
-    proj = acc[...].astype(jnp.bfloat16)
-    rows_b[0] = rotate(proj[:, :head_dim], cos_b[...], sin_b[...]).astype(jnp.float32)
-    rows_b[1] = rotate(proj[:, head_dim:2 * head_dim], cos_b[...], sin_b[...]).astype(jnp.float32)
-    rows_b[2] = proj[:, 2 * head_dim:].astype(jnp.float32)
-
-    slot_of = lax.broadcasted_iota(jnp.int32, (slots_heads, head_dim), 0) // heads
-    pair = lax.broadcasted_iota(jnp.int32, (heads, slots_heads), 1)
-    same = pair % heads == lax.broadcasted_iota(jnp.int32, (heads, slots_heads), 0)
-
-    def attend(b, carry):
-        length = c_len[b]
-        mine = pl.ds(pl.multiple_of(b * heads, heads), heads)
-
-        def updated(buf, new):
-            wide = jnp.broadcast_to(new[None], (slots_heads // heads, heads, head_dim)).reshape(slots_heads, head_dim)
-            return jnp.where(slot_of == length, wide, buf[b].astype(jnp.float32)).astype(jnp.bfloat16)
-        pltpu.make_async_copy(k_cache.at[b], k_buf.at[b], k_in.at[b]).wait()
-        k_buf[b] = updated(k_buf, rows_b[1, mine])
-        pltpu.make_async_copy(v_cache.at[b], v_buf.at[b], v_in.at[b]).wait()
-        v_buf[b] = updated(v_buf, rows_b[2, mine])
-        pltpu.make_async_copy(k_buf.at[b], k_new.at[b], k_sem.at[b]).start()
-        pltpu.make_async_copy(v_buf.at[b], v_new.at[b], v_sem.at[b]).start()
-        scores = lax.dot_general(rows_b[0, mine].astype(jnp.bfloat16), k_buf[b], dims, preferred_element_type=jnp.float32) * scale
-        scores = jnp.where(same & (pair // heads <= length), scores, -1e30)
-        expd = jnp.exp(scores - jnp.max(scores, axis=-1, keepdims=True))
-        prob = (expd / jnp.sum(expd, axis=-1, keepdims=True)).astype(jnp.bfloat16)
-        attn_b[b] = jnp.dot(prob, v_buf[b], preferred_element_type=jnp.float32).astype(jnp.bfloat16)
-        return carry
-    lax.fori_loop(0, dec_rows, attend, 0)
-
-    def cache_out(b, carry):
-        pltpu.make_async_copy(k_buf.at[b], k_new.at[b], k_sem.at[b]).wait()
-        pltpu.make_async_copy(v_buf.at[b], v_new.at[b], v_sem.at[b]).wait()
-        return carry
-    lax.fori_loop(0, dec_rows, cache_out, 0)
+        for b in range(h * dec_rows // heads, (h + 1) * dec_rows // heads):
+            for copy in cache_in(b):
+                copy.wait()
+            for copy in cache_out(b):
+                copy.start()
+    for b in range(dec_rows):
+        for copy in cache_out(b):
+            copy.wait()
+
+
+def insert_kernel(c_len, fresh, k_old, v_old, k_new, v_new, row_buf, row_sem):
+    dec_rows, heads, head_dim = row_buf.shape[1:]
+    del k_old, v_old
+    for which in range(2):
+        for b in range(dec_rows):
+            row_buf[which, b] = fresh[which, b * heads:(b + 1) * heads, :].astype(jnp.bfloat16)
+
+    def copies(b):
+        place = pl.ds(pl.multiple_of(c_len[b] * heads, heads), heads)
+        return [pltpu.make_async_copy(row_buf.at[which, b], dst.at[b, place, :], row_sem.at[which, b]) for which, dst in enumerate((k_new, v_new))]
+    for b in range(dec_rows):
+        for copy in copies(b):
+            copy.start()
+    for b in range(dec_rows):
+        for copy in copies(b):
+            copy.wait()
+
+
+def insert_call(c_len, fresh, k_copy, v_copy):
+    dec_rows = k_copy.shape[0]
+    head_dim = k_copy.shape[2]
+    heads = fresh.shape[1] // dec_rows
+    hbm = pl.BlockSpec(memory_space=pl.ANY)
+    return pl.pallas_call(
+        insert_kernel,
+        out_shape=(jax.ShapeDtypeStruct(k_copy.shape, k_copy.dtype),) * 2,
+        in_specs=[pl.BlockSpec(memory_space=pltpu.SMEM), pl.BlockSpec(memory_space=pltpu.VMEM), hbm, hbm],
+        out_specs=(hbm, hbm),
+        scratch_shapes=[pltpu.VMEM((2, dec_rows, heads, head_dim), jnp.bfloat16), pltpu.SemaphoreType.DMA((2, dec_rows))],
+        input_output_aliases={2: 0, 3: 1},
+        compiler_params=pltpu.CompilerParams(vmem_limit_bytes=62 * 1024 * 1024),
+        name='insert',
+    )(c_len, fresh, k_copy, v_copy)
 
 
 def rope_tables(positions, head_dim):
@@ -510,48 +585,37 @@
     return jnp.concatenate([cos_tab, cos_tab], axis=-1), jnp.concatenate([-sin_tab, sin_tab], axis=-1)
 
 
-def front_call(x_rows, y_rows, s_len, c_len, w_qkv_a, w_qkv_b, gain_a, gain_b, k_cache, v_cache, tp_size):
+def decode_operands(y_rows, c_len, gain_b, heads, head_dim):
+    dec_rows, width = y_rows.shape
+    span = 256 // heads
+    slices_b = jnp.transpose(rms_norm(y_rows, gain_b).reshape(dec_rows, width // span, span), (1, 0, 2)).reshape(-1, span)
+    cos_b, sin_b = (jnp.repeat(tab, heads, axis=0) for tab in rope_tables(c_len, head_dim))
+    return slices_b, cos_b, sin_b
+
+
+def front_call(x_rows, s_len, w_qkv_a, gain_a, k_cache, v_cache, tp_size):
     num_rows, width = x_rows.shape
-    dec_rows = y_rows.shape[0]
     heads, wide = w_qkv_a.shape[1:]
-    head_dim = k_cache.shape[-1]
-    cache_rows = k_cache.shape[1] * heads
+    dec_rows, cache_rows, head_dim = k_cache.shape
     qkv_a = jnp.einsum('sd,dhe->she', rms_norm(x_rows, gain_a), w_qkv_a, preferred_element_type=jnp.float32).astype(jnp.bfloat16)
     qkv_a = jnp.transpose(qkv_a, (1, 0, 2))
-    lanes = 256
-    span = lanes // heads
-    slices_b = jnp.transpose(rms_norm(y_rows, gain_b).reshape(dec_rows, width // span, span), (1, 0, 2)).reshape(-1, span)
     cos_a, sin_a = rope_tables(jnp.arange(num_rows), head_dim)
-    cos_b, sin_b = (jnp.repeat(tab, heads, axis=0) for tab in rope_tables(c_len, head_dim))
     vmem = pl.BlockSpec(memory_space=pltpu.VMEM)
-    smem = pl.BlockSpec(memory_space=pltpu.SMEM)
     hbm = pl.BlockSpec(memory_space=pl.ANY)
     dma = pltpu.SemaphoreType.DMA
-    depth = 2048
-    fold = heads // tp_size * head_dim
     bf16 = jnp.bfloat16
     cache = jax.ShapeDtypeStruct((dec_rows, cache_rows, head_dim), bf16)
-    moved = jax.ShapeDtypeStruct((tp_size, num_rows, fold), bf16)
+    moved = jax.ShapeDtypeStruct((tp_size, num_rows, heads // tp_size * head_dim), bf16)
     return pl.pallas_call(
         front_kernel,
-        out_shape=(jax.ShapeDtypeStruct((num_rows, heads * head_dim), bf16), moved, moved,
-                   jax.ShapeDtypeStruct((dec_rows, heads, head_dim), bf16), cache, cache),
-        in_specs=[smem] * 2 + [vmem] * 6 + [hbm] * 3,
-        out_specs=(vmem, vmem, vmem, vmem, hbm, hbm),
-        scratch_shapes=[
-            pltpu.VMEM((dec_rows, cache_rows, head_dim), bf16),
-            pltpu.VMEM((dec_rows, cache_rows, head_dim), bf16),
-            pltpu.VMEM((FRONT_RING, depth, wide), bf16),
-            pltpu.VMEM((width // span * dec_rows, lanes), jnp.float32),
-            pltpu.VMEM((dec_rows * heads, wide), jnp.float32),
-            pltpu.VMEM((3, dec_rows * heads, head_dim), jnp.float32),
-            dma((dec_rows,)), dma((dec_rows,)), dma((dec_rows,)), dma((dec_rows,)), dma((FRONT_RING,)),
-        ],
+        out_shape=(jax.ShapeDtypeStruct((num_rows, heads * head_dim), bf16), moved, moved, cache, cache),
+        in_specs=[pl.BlockSpec(memory_space=pltpu.SMEM)] + [vmem] * 3 + [hbm] * 2,
+        out_specs=(vmem, vmem, vmem, hbm, hbm),
+        scratch_shapes=[pltpu.VMEM(cache.shape, bf16)] * 2 + [dma((dec_rows,))] * 4,
         compiler_params=pltpu.CompilerParams(vmem_limit_bytes=62 * 1024 * 1024),
-        cost_estimate=pl.CostEstimate(flops=2 * width * heads * wide * dec_rows, bytes_accessed=60000000, transcendentals=0),
+        cost_estimate=pl.CostEstimate(flops=8 * num_rows * num_rows * heads * head_dim, bytes_accessed=8 * k_cache.size, transcendentals=0),
         name='front',
-    )(s_len, c_len, qkv_a, cos_a, sin_a, slices_b, cos_b, sin_b, w_qkv_b.reshape(width * heads, wide),
-      k_cache.reshape(dec_rows, cache_rows, head_dim), v_cache.reshape(dec_rows, cache_rows, head_dim))
+    )(s_len, qkv_a, cos_a, sin_a, k_cache, v_cache)
 
 
 def solution(mesh):
@@ -570,13 +634,16 @@
         width = x_prompt.shape[1]
         head_dim = k_cache.shape[-1]
         dec_rows, slots, heads = k_cache.shape[1:4]
-        attn_a, keys, vals, attn_b, k_new, v_new = front_call(
-            x_prompt, y_tok, s_len, c_len, wqkv_a[0], wqkv_b[0, :, :, 0], norm_a[0, 0], norm_b[0, 0],
-            k_cache[0, :, :, :, 0], v_cache[0, :, :, :, 0], tp_size)
-        hidden, y_out, k_prompt, v_prompt = block_call(
-            x_prompt, y_tok, attn_a, attn_b.reshape(dec_rows, -1), norm_a[0, 1:2], norm_b[0, 1:2],
+        k_rows = k_cache.reshape(dec_rows, slots * heads, head_dim)
+        v_rows = v_cache.reshape(dec_rows, slots * heads, head_dim)
+        attn_a, keys, vals, k_copy, v_copy = front_call(x_prompt, s_len, wqkv_a[0], norm_a[0, 0], k_rows, v_rows, tp_size)
+        slices_b, cos_b, sin_b = decode_operands(y_tok, c_len, norm_b[0, 0], heads, head_dim)
+        hidden, y_out, k_prompt, v_prompt, fresh = block_call(
+            c_len, x_prompt, y_tok, attn_a, slices_b, cos_b, sin_b, norm_a[0, 1:2], norm_b[0, 1:2],
             wo_a[0].reshape(-1, width), jnp.transpose(wug_a[0], (1, 2, 0)), wd_a[0],
-            wo_b[0].reshape(-1, width), jnp.transpose(wug_b[0], (1, 2, 0)), wd_b[0], keys, vals)
+            wo_b[0].reshape(-1, width), jnp.transpose(wug_b[0], (1, 2, 0)), wd_b[0], keys, vals,
+            wqkv_b.reshape(width * heads, -1), k_rows, v_rows)
+        k_new, v_new = insert_call(c_len, fresh, k_copy, v_copy)
         prompt_shape = (1, x_prompt.shape[0], heads, 1, head_dim)
         return (hidden, y_out, k_prompt.reshape(prompt_shape), v_prompt.reshape(prompt_shape),
                 k_new.reshape(k_cache.shape), v_new.reshape(v_cache.shape))

time: 268 us -> 258 us (0.963)
  Pallas kernels: 232 us -> 225 us
  local copies, waits for them, and re-layouts: 11.3 us -> 7.86 us
    pallas_call x1, Pallas kernels: 21.2 us -> 9.56 us  [front_call(): pl.pallas_call(front_kernel, out_shape=(jax.ShapeDtypeStruct((num_rows, h...]
    unnamed x9 -> x12, local copies, waits for them, and re-layouts: 9 us -> 5.57 us
    pallas_call x1, Pallas kernels: 211 us -> 214 us  [block_call(): pl.pallas_call(block_kernel, out_shape=(jax.ShapeDtypeStruct((rows, width...]
where the time goes in v4:
time: 258 us; the launch traced here: 257 us
  Pallas kernels  225 us (87%)
  matrix products  15.1 us (6%)
  local copies, waits for them, and re-layouts  7.86 us (3%)
  other arithmetic  7.73 us (3%)
    pallas_call x1, Pallas kernels, block_call(): pl.pallas_call(block_kernel, out_shape=(jax.ShapeDtypeStruct((rows, width...  214 us
    dot_general x1, matrix products, front_call(): jnp.einsum('sd,dhe->she', rms_norm(x_rows, gain_a), w_qkv_a, preferred_el...  15.1 us
    pallas_call x1, Pallas kernels, front_call(): pl.pallas_call(front_kernel, out_shape=(jax.ShapeDtypeStruct((num_rows, h...  9.56 us
    unnamed x12, local copies, waits for them, and re-layouts  5.57 us

profile of v4, /device:TPU:0, one launch (start us, length us, event | category | flops | bytes accessed | tf_op | source)
XLA Modules:
  0.0 257.4 jit_solution(8824480765170133075)
XLA Ops:
  0.6 0.0 copy-start
  1.5 1.0 fusion.19
  2.4 0.7 convert_element_type.66
  3.1 2.1 fusion.2
  5.2 0.1 fusion.23
  5.3 0.1 pad_maximum_fusion.2
  5.4 0.6 broadcast_bitcast_fusion.1.cos_b
  6.0 0.6 broadcast_bitcast_fusion.sin_b
  6.6 1.5 slice_bitcast_fusion
  8.1 0.9 fusion.21
  9.0 0.2 reshape.88
  9.2 0.9 copy.45
  10.1 0.5 fusion.22
  10.7 0.8 pad_maximum_fusion
  11.5 0.0 copy-done
  11.5 15.1 %fusion.14.qkv_a = bf16[8,256,384]{2,1,0:T(8,128)(2,1)} fusion(bf16[4096,8,384]{2,1,0:T(8,128)(2,1)} %bitcast.76, bf16[256,4096]{1,0:T(8,128)(2,1)S(1)} %copy-done, f32[4096]{0:T(1024)S(1)} %bitcast.75, f32[256]{0:T(256)S(1)} %add_rsqrt_fusion), kind=kOutput, calls=%fused_computation.11 | convolution fusion | flops 6447431680 | bytes 28853248 | tf_op jit(solution)/shard_map/sd,dhe->she/dot_general | solution.py:600
  26.6 9.6 %front.1 = (bf16[256,1024]{1,0:T(8,128)(2,1)}, bf16[4,256,256]{2,1,0:T(8,128)(2,1)}, bf16[4,256,256]{2,1,0:T(8,128)(2,1)}, bf16[8,2048,128]{2,1,0:T(8,128)(2,1)}, bf16[8,2048,128]{2,1,0:T(8,128)(2,1)}) custom-call(s32[1]{0:T(128)S(6)} %copy.50.s_len, bf16[8,256,384]{2,1,0:T(8,128)(2,1)} %fusion.14.qkv_a, f32[256,128]{1,0:T(8,128)} %get-tuple-element.52.cos_a, ...), custom_call_target="tpu_custom_call" | custom-call | flops 536870912 | bytes 16777216 | tf_op jit(solution)/shard_map/front/pallas_call | solution.py:609
  36.2 213.9 %block.1 = (bf16[256,4096]{1,0:T(8,128)(2,1)}, bf16[8,4096]{1,0:T(8,128)(2,1)}, bf16[256,1024]{1,0:T(8,128)(2,1)}, bf16[256,1024]{1,0:T(8,128)(2,1)}, f32[2,64,128]{2,1,0:T(8,128)}) custom-call(s32[8]{0:T(128)} %c_len.3, bf16[256,4096]{1,0:T(8,128)(2,1)} %x_ref.1, bf16[8,4096]{1,0:T(8,128)(2,1)} %y_ref.1, bf16[256,1024]{1,0:T(8,128)(2,1)} %get-tuple-element.18.attn_a_ref, ...), custom_call_target="tpu_custom_call" | custom-call | flops 10034872320 | bytes 228065280 | tf_op jit(solution)/shard_map/block/pallas_call | solution.py:456
  250.0 0.0 copy-start.2
  250.1 1.7 insert.1
  251.8 0.9 copy.36
  252.7 0.9 copy.37
  253.6 3.1 %copy.51 = bf16[256,4096]{1,0:T(8,128)(2,1)} copy(bf16[256,4096]{1,0:T(8,128)(2,1)} %get-tuple-element.64) | data formatting | bytes 4194304
  256.7 0.6 copy.52
  (9 shorter events, 0.0 us)
Async XLA Ops:
  0.6 10.9 %copy-start = (bf16[256,4096]{1,0:T(8,128)(2,1)S(1)}, bf16[256,4096]{1,0:T(8,128)(2,1)}, u32[]{:S(2)}) copy-start(bf16[256,4096]{1,0:T(8,128)(2,1)} %x_ref.1) | copy-start | bytes 6291460
  250.0 1.8 copy-start.2
  250.0 2.7 %copy-start.1 = (bf16[256,1024]{1,0:T(8,128)(2,1)S(1)}, bf16[256,1024]{1,0:T(8,128)(2,1)}, u32[]{:S(2)}) copy-start(bf16[256,1024]{1,0:T(8,128)(2,1)} %get-tuple-element.24) | copy-start | bytes 1572868
  251.8 4.9 %copy-start.3 = (bf16[8,4096]{1,0:T(8,128)(2,1)S(1)}, bf16[8,4096]{1,0:T(8,128)(2,1)}, u32[]{:S(2)}) copy-start(bf16[8,4096]{1,0:T(8,128)(2,1)} %get-tuple-element.65) | copy-start | bytes 196612

commit v5 on v4

--- a/solution.py
+++ b/solution.py
@@ -1,5 +1,6 @@
 import jax
 import jax.numpy as jnp
+import numpy as np
 from jax import lax
 from jax.experimental import pallas as pl
 from jax.experimental.pallas import tpu as pltpu
@@ -37,7 +38,7 @@
 RATE = 1
 
 
-def block_kernel(c_len, x_ref, y_ref, attn_a_ref, slices_b, cos_b, sin_b, norm_a_ref, norm_b_ref, wo_a, wug_a, wd_a, wo_b, wug_b, wd_b, keys, vals, wqkv_b, k_cache, v_cache,
+def block_kernel(c_len, x_ref, y_ref, attn_a_ref, cos_tab, sin_tab, norm_a_ref, norm_b_ref, wo_a, wug_a, wd_a, wo_b, wug_b, wd_b, keys, vals, wqkv_b, k_cache, v_cache,
                  out_a, out_b, k_out, v_out, fresh,
                  part, rcv, hid, part_d, rcv_d, hid_d, normed, act, normed_d, act_d, ug_buf, dn_buf,
                  rs_send, rs_recv, ag_send, ag_recv, rsd_send, rsd_recv, agd_send, agd_recv, ug_sem, dn_sem, out_sem, hand_send, hand_recv,
@@ -242,7 +243,7 @@
 
             def scale(q, carry, load=load, inv=inv, r=r):
                 cols = pl.ds(pl.multiple_of(q * WIRE, WIRE), WIRE)
-                normed[r * WIRE_ROWS:(r + 1) * WIRE_ROWS, cols] = (load(q) * inv * norm_a_ref[:, cols].astype(jnp.float32)).astype(jnp.bfloat16)
+                normed[r * WIRE_ROWS:(r + 1) * WIRE_ROWS, cols] = (load(q) * inv * norm_a_ref[1:2, cols].astype(jnp.float32)).astype(jnp.bfloat16)
                 return carry
             lax.fori_loop(0, 2 * blocks, scale, 0)
 
@@ -270,7 +271,7 @@
     for slot in range(RING):
         dn_copy(wo_a, slot, slot).start()
     heads = wqkv_b.shape[0] // width
-    head_dim = cos_b.shape[1]
+    head_dim = cos_tab.shape[1]
     dec_rows, slots_heads, _ = k_cache.shape
     w_depth = w_buf.shape[1]
     n_w = wqkv_b.shape[0] // w_depth
@@ -323,11 +324,28 @@
 
     lanes = spread.shape[1]
     span = lanes // heads
-    one = (lax.broadcasted_iota(jnp.int32, (span, lanes), 1) // heads == lax.broadcasted_iota(jnp.int32, (span, lanes), 0))
-    spread[...] = jnp.dot(slices_b[...], jnp.where(one, 1.0, 0.0).astype(jnp.bfloat16), preferred_element_type=jnp.float32)
+    group = 4
+    one = (lax.broadcasted_iota(jnp.int32, (group * span, group * lanes), 1) // heads == lax.broadcasted_iota(jnp.int32, (group * span, group * lanes), 0))
+    one = jnp.where(one, 1.0, 0.0).astype(jnp.bfloat16)
+    val = y_ref[...].astype(jnp.float32)
+    inv = lax.rsqrt(jnp.mean(val * val, axis=-1, keepdims=True) + NORM_EPS)
+    normed_d[...] = (val * inv * norm_b_ref[0:1, :].astype(jnp.float32)).astype(jnp.bfloat16)
+    n_spread = width // (group * span)
+    first_slots = 8
+
+    def widen(i, carry):
+        for e in range(n_spread // first_slots):
+            at = i * (n_spread // first_slots) + e
+            cols = pl.ds(pl.multiple_of(at * group * span, group * span), group * span)
+            block = jnp.dot(normed_d[:, cols], one, preferred_element_type=jnp.float32)
+            for q in range(group):
+                spread[pl.ds(pl.multiple_of((at * group + q) * dec_rows, dec_rows), dec_rows), :] = block[:, q * lanes:(q + 1) * lanes]
+        slot_step(i, *flow_one)
+        return carry
+    lax.fori_loop(0, first_slots, widen, 0)
     acc[...] = jnp.zeros_like(acc)
     inner = w_depth // lanes
-    early = beside(0, n_w, flow_one, 1)
+    early = beside(first_slots, first_slots + n_w, flow_one, 1)
 
     def project(i, carry):
         own = lax.broadcasted_iota(jnp.int32, (dec_rows, heads, lanes), 2) % heads == lax.broadcasted_iota(jnp.int32, (dec_rows, heads, lanes), 1)
@@ -350,8 +368,11 @@
     def rotate(val):
         val = val.astype(jnp.float32)
         swapped = jnp.concatenate([val[:, head_dim // 2:], val[:, :head_dim // 2]], axis=-1)
-        return (val * cos_b[...] + swapped * sin_b[...]).astype(jnp.bfloat16).astype(jnp.float32)
-
+        return (val * cos_b + swapped * sin_b).astype(jnp.bfloat16).astype(jnp.float32)
+
+    def by_row(tab):
+        return jnp.concatenate([jnp.broadcast_to(tab[pl.ds(c_len[b], 1), :], (heads, head_dim)) for b in range(dec_rows)], axis=0)
+    cos_b, sin_b = by_row(cos_tab), by_row(sin_tab)
     proj = acc[...].astype(jnp.bfloat16)
     rows_b[0] = rotate(proj[:, :head_dim])
     rows_b[1] = rotate(proj[:, head_dim:2 * head_dim])
@@ -359,7 +380,7 @@
     fresh[0] = rows_b[1]
     fresh[1] = rows_b[2]
 
-    late = beside(n_w, n_w + dec_rows, flow_one, 1)
+    late = beside(first_slots + n_w, first_slots + n_w + dec_rows, flow_one, 1)
 
     def attend(b, carry):
         length = c_len[b]
@@ -392,7 +413,7 @@
 
     def dec_proj(j, slot):
         put_dec(0, j, jnp.dot(attn_b, dn_buf[slot, :heads * head_dim, :], preferred_element_type=jnp.float32))
-    first = n_w + dec_rows
+    first = first_slots + n_w + dec_rows
     dn_phase(wo_b, wd_a, n_dn, dec_proj, beside(first, min(first + n_dn, dec_one), flow_one, 1))
     slots(min(first + n_dn, dec_one), per + depth, flow_one)
 
@@ -409,7 +430,7 @@
 
     val = jnp.concatenate([hid_d[0, 0], hid_d[0, 1]], axis=-1).astype(jnp.float32)
     inv = lax.rsqrt(jnp.mean(val * val, axis=-1, keepdims=True) + NORM_EPS)
-    normed_d[...] = (val * inv * norm_b_ref[...].astype(jnp.float32)).astype(jnp.bfloat16)
+    normed_d[...] = (val * inv * norm_b_ref[1:2, :].astype(jnp.float32)).astype(jnp.bfloat16)
     up_phase(wug_b, None, 2 * n_up, normed_d, act_d, beside(per, per + RATE * n_up, flow_c1, RATE))
     dn_phase(wd_b, None, 4 * n_dn, lambda j, slot: put_dec(1, j, down_dot(act_d, slot)), beside(per + RATE * n_up, dec_two, flow_c1, RATE))
     slots(dec_two, max(2 * per, dec_two + 1) + depth, flow_c1)
@@ -441,9 +462,10 @@
         pltpu.make_async_copy(hid.at[half, pl.ds(0, 2 * per)], hid.at[half, pl.ds(2 * per, 2 * per)], out_sem.at[half]).wait()
 
 
-def block_call(c_len, x_rows, y_rows, attn_a, slices_b, cos_b, sin_b, norm_a, norm_b, wo_a, wug_a, wd_a, wo_b, wug_b, wd_b, keys, vals, wqkv_b, k_cache, v_cache):
+def block_call(c_len, x_rows, y_rows, attn_a, cos_tab, sin_tab, norm_a, norm_b, wo_a, wug_a, wd_a, wo_b, wug_b, wd_b, keys, vals, wqkv_b, k_cache, v_cache):
     rows, width = x_rows.shape
     dec_rows = y_rows.shape[0]
+    heads, head_dim = wqkv_b.shape[0] // width, cos_tab.shape[1]
     ffn = wd_a.shape[0]
     mid = width // 2
     cuts = HALF_ROWS // WIRE_ROWS
@@ -457,8 +479,8 @@
         block_kernel,
         out_shape=(jax.ShapeDtypeStruct((rows, width), jnp.bfloat16), jax.ShapeDtypeStruct((dec_rows, width), jnp.bfloat16),
                    *[jax.ShapeDtypeStruct((rows, keys.shape[0] * keys.shape[2]), jnp.bfloat16)] * 2,
-                   jax.ShapeDtypeStruct((2,) + cos_b.shape, jnp.float32)),
-        in_specs=[pl.BlockSpec(memory_space=pltpu.SMEM)] + [vmem] * 8 + [hbm] * 11,
+                   jax.ShapeDtypeStruct((2, dec_rows * heads, head_dim), jnp.float32)),
+        in_specs=[pl.BlockSpec(memory_space=pltpu.SMEM)] + [vmem] * 7 + [hbm] * 11,
         out_specs=(hbm, vmem, hbm, hbm, vmem),
         scratch_shapes=[
             pltpu.VMEM((2, 4 * per, WIRE_ROWS, WIRE), jnp.float32),
@@ -479,16 +501,16 @@
             pltpu.VMEM((2,) + k_cache.shape[1:], jnp.bfloat16),
             pltpu.VMEM((2,) + k_cache.shape[1:], jnp.bfloat16),
             pltpu.VMEM((RING, 2048, wqkv_b.shape[1]), jnp.bfloat16),
-            pltpu.VMEM((slices_b.shape[0], 256), jnp.float32),
-            pltpu.VMEM((cos_b.shape[0], wqkv_b.shape[1]), jnp.float32),
-            pltpu.VMEM((3,) + cos_b.shape, jnp.float32),
-            pltpu.VMEM((dec_rows, cos_b.shape[0] // dec_rows, cos_b.shape[1]), jnp.float32),
+            pltpu.VMEM((width * heads // 256 * dec_rows, 256), jnp.float32),
+            pltpu.VMEM((dec_rows * heads, wqkv_b.shape[1]), jnp.float32),
+            pltpu.VMEM((3, dec_rows * heads, head_dim), jnp.float32),
+            pltpu.VMEM((dec_rows, heads, head_dim), jnp.float32),
             dma((2,)), dma((2,)), dma((RING,)),
         ],
         compiler_params=pltpu.CompilerParams(collective_id=0, has_side_effects=True, vmem_limit_bytes=62 * 1024 * 1024),
         cost_estimate=pl.CostEstimate(flops=weights * (rows + dec_rows) // 2, bytes_accessed=weights * 3, transcendentals=0),
         name='block',
-    )(c_len, x_rows, y_rows, attn_a, slices_b, cos_b, sin_b, norm_a, norm_b, wo_a, wug_a, wd_a, wo_b, wug_b, wd_b, keys, vals, wqkv_b, k_cache, v_cache)
+    )(c_len, x_rows, y_rows, attn_a, cos_tab, sin_tab, norm_a, norm_b, wo_a, wug_a, wd_a, wo_b, wug_b, wd_b, keys, vals, wqkv_b, k_cache, v_cache)
 
 
 def front_kernel(s_len, qkv_a, cos_a, sin_a, k_cache, v_cache, attn_a, keys, vals, k_new, v_new, k_buf, v_buf, k_in, v_in, k_sem, v_sem):
@@ -542,9 +564,20 @@
             copy.wait()
 
 
-def insert_kernel(c_len, fresh, k_old, v_old, k_new, v_new, row_buf, row_sem):
+def insert_kernel(c_len, fresh, y_in, hid_in, k_old, v_old, k_new, v_new, hid_out, y_out, row_buf, row_sem, hid_buf, in_sem, out_sem):
     dec_rows, heads, head_dim = row_buf.shape[1:]
     del k_old, v_old
+    pieces = in_sem.shape[0]
+    depth = hid_in.shape[0] // pieces
+
+    def piece_in(i):
+        return pltpu.make_async_copy(hid_in.at[pl.ds(i * depth, depth), :], hid_buf.at[pl.ds(i * depth, depth), :], in_sem.at[i])
+
+    def piece_out(i):
+        return pltpu.make_async_copy(hid_buf.at[pl.ds(i * depth, depth), :], hid_out.at[pl.ds(i * depth, depth), :], out_sem.at[i])
+    for i in range(pieces):
+        piece_in(i).start()
+    y_out[...] = y_in[...]
     for which in range(2):
         for b in range(dec_rows):
             row_buf[which, b] = fresh[which, b * heads:(b + 1) * heads, :].astype(jnp.bfloat16)
@@ -555,51 +588,50 @@
     for b in range(dec_rows):
         for copy in copies(b):
             copy.start()
+    for i in range(pieces):
+        piece_in(i).wait()
+        piece_out(i).start()
     for b in range(dec_rows):
         for copy in copies(b):
             copy.wait()
-
-
-def insert_call(c_len, fresh, k_copy, v_copy):
+    for i in range(pieces):
+        piece_out(i).wait()
+
+
+def insert_call(c_len, fresh, y_in, hid_in, k_copy, v_copy):
     dec_rows = k_copy.shape[0]
     head_dim = k_copy.shape[2]
     heads = fresh.shape[1] // dec_rows
     hbm = pl.BlockSpec(memory_space=pl.ANY)
+    vmem = pl.BlockSpec(memory_space=pltpu.VMEM)
     return pl.pallas_call(
         insert_kernel,
-        out_shape=(jax.ShapeDtypeStruct(k_copy.shape, k_copy.dtype),) * 2,
-        in_specs=[pl.BlockSpec(memory_space=pltpu.SMEM), pl.BlockSpec(memory_space=pltpu.VMEM), hbm, hbm],
-        out_specs=(hbm, hbm),
-        scratch_shapes=[pltpu.VMEM((2, dec_rows, heads, head_dim), jnp.bfloat16), pltpu.SemaphoreType.DMA((2, dec_rows))],
-        input_output_aliases={2: 0, 3: 1},
+        out_shape=(jax.ShapeDtypeStruct(k_copy.shape, k_copy.dtype),) * 2 + (jax.ShapeDtypeStruct(hid_in.shape, hid_in.dtype), jax.ShapeDtypeStruct(y_in.shape, y_in.dtype)),
+        in_specs=[pl.BlockSpec(memory_space=pltpu.SMEM), vmem, vmem, hbm, hbm, hbm],
+        out_specs=(hbm, hbm, hbm, vmem),
+        scratch_shapes=[pltpu.VMEM((2, dec_rows, heads, head_dim), jnp.bfloat16), pltpu.SemaphoreType.DMA((2, dec_rows)),
+                        pltpu.VMEM(hid_in.shape, hid_in.dtype), pltpu.SemaphoreType.DMA((4,)), pltpu.SemaphoreType.DMA((4,))],
+        input_output_aliases={4: 0, 5: 1},
         compiler_params=pltpu.CompilerParams(vmem_limit_bytes=62 * 1024 * 1024),
         name='insert',
-    )(c_len, fresh, k_copy, v_copy)
-
-
-def rope_tables(positions, head_dim):
+    )(c_len, fresh, y_in, hid_in, k_copy, v_copy)
+
+
+def rope_tables(count, head_dim):
     half_dim = head_dim // 2
-    inv_freq = ROPE_BASE ** (-jnp.arange(half_dim, dtype=jnp.float32) / half_dim)
-    angles = positions.astype(jnp.float32)[:, None] * inv_freq[None, :]
-    cos_tab, sin_tab = jnp.cos(angles), jnp.sin(angles)
-    return jnp.concatenate([cos_tab, cos_tab], axis=-1), jnp.concatenate([-sin_tab, sin_tab], axis=-1)
-
-
-def decode_operands(y_rows, c_len, gain_b, heads, head_dim):
-    dec_rows, width = y_rows.shape
-    span = 256 // heads
-    slices_b = jnp.transpose(rms_norm(y_rows, gain_b).reshape(dec_rows, width // span, span), (1, 0, 2)).reshape(-1, span)
-    cos_b, sin_b = (jnp.repeat(tab, heads, axis=0) for tab in rope_tables(c_len, head_dim))
-    return slices_b, cos_b, sin_b
-
-
-def front_call(x_rows, s_len, w_qkv_a, gain_a, k_cache, v_cache, tp_size):
+    inv_freq = np.float32(ROPE_BASE) ** (-np.arange(half_dim, dtype=np.float32) / np.float32(half_dim))
+    angles = np.arange(count, dtype=np.float32)[:, None] * inv_freq.astype(np.float32)[None, :]
+    cos_tab, sin_tab = np.cos(angles.astype(np.float64)), np.sin(angles.astype(np.float64))
+    both = np.concatenate([cos_tab, cos_tab], axis=-1), np.concatenate([-sin_tab, sin_tab], axis=-1)
+    return tuple(jnp.asarray(tab.astype(np.float32)) for tab in both)
+
+
+def front_call(x_rows, s_len, w_qkv_a, gain_a, k_cache, v_cache, cos_a, sin_a, tp_size):
     num_rows, width = x_rows.shape
     heads, wide = w_qkv_a.shape[1:]
     dec_rows, cache_rows, head_dim = k_cache.shape
     qkv_a = jnp.einsum('sd,dhe->she', rms_norm(x_rows, gain_a), w_qkv_a, preferred_element_type=jnp.float32).astype(jnp.bfloat16)
     qkv_a = jnp.transpose(qkv_a, (1, 0, 2))
-    cos_a, sin_a = rope_tables(jnp.arange(num_rows), head_dim)
     vmem = pl.BlockSpec(memory_space=pltpu.VMEM)
     hbm = pl.BlockSpec(memory_space=pl.ANY)
     dma = pltpu.SemaphoreType.DMA
@@ -636,14 +668,14 @@
         dec_rows, slots, heads = k_cache.shape[1:4]
         k_rows = k_cache.reshape(dec_rows, slots * heads, head_dim)
         v_rows = v_cache.reshape(dec_rows, slots * heads, head_dim)
-        attn_a, keys, vals, k_copy, v_copy = front_call(x_prompt, s_len, wqkv_a[0], norm_a[0, 0], k_rows, v_rows, tp_size)
-        slices_b, cos_b, sin_b = decode_operands(y_tok, c_len, norm_b[0, 0], heads, head_dim)
+        cos_tab, sin_tab = rope_tables(max(slots, x_prompt.shape[0]), head_dim)
+        attn_a, keys, vals, k_copy, v_copy = front_call(x_prompt, s_len, wqkv_a[0], norm_a[0, 0], k_rows, v_rows, cos_tab, sin_tab, tp_size)
         hidden, y_out, k_prompt, v_prompt, fresh = block_call(
-            c_len, x_prompt, y_tok, attn_a, slices_b, cos_b, sin_b, norm_a[0, 1:2], norm_b[0, 1:2],
+            c_len, x_prompt, y_tok, attn_a, cos_tab, sin_tab, norm_a[0], norm_b[0],
             wo_a[0].reshape(-1, width), jnp.transpose(wug_a[0], (1, 2, 0)), wd_a[0],
             wo_b[0].reshape(-1, width), jnp.transpose(wug_b[0], (1, 2, 0)), wd_b[0], keys, vals,
             wqkv_b.reshape(width * heads, -1), k_rows, v_rows)
-        k_new, v_new = insert_call(c_len, fresh, k_copy, v_copy)
+        k_new, v_new, hidden, y_out = insert_call(c_len, fresh, y_out, hidden, k_copy, v_copy)
         prompt_shape = (1, x_prompt.shape[0], heads, 1, head_dim)
         return (hidden, y_out, k_prompt.reshape(prompt_shape), v_prompt.reshape(prompt_shape),
                 k_new.reshape(k_cache.shape), v_new.reshape(v_cache.shape))

time: 258 us -> 251 us (0.973)
  local copies, waits for them, and re-layouts: 7.86 us -> 1.8 us
  other arithmetic: 7.73 us -> 2.83 us
    unnamed x12 -> x6, local copies, waits for them, and re-layouts: 5.57 us -> 1.8 us
where the time goes in v5:
time: 251 us; the launch traced here: 250 us
  Pallas kernels  227 us (90%)
  matrix products  17.4 us (7%)
  other arithmetic  2.83 us (1%)
    pallas_call x1, Pallas kernels, block_call(): pl.pallas_call(block_kernel, out_shape=(jax.ShapeDtypeStruct((rows, width...  213 us
    dot_general x1, matrix products, front_call(): jnp.einsum('sd,dhe->she', rms_norm(x_rows, gain_a), w_qkv_a, preferred_el...  17.4 us
    pallas_call x1, Pallas kernels, front_call(): pl.pallas_call(front_kernel, out_shape=(jax.ShapeDtypeStruct((num_rows, h...  9.54 us

profile of v5, /device:TPU:0, one launch (start us, length us, event | category | flops | bytes accessed | tf_op | source)
XLA Modules:
  0.0 250.3 jit_solution(15780607363169238628)
XLA Ops:
  1.3 2.1 fusion.2
  3.4 0.7 slice_convert_fusion
  4.1 17.4 %fusion.14.qkv_a = bf16[8,256,384]{2,1,0:T(8,128)(2,1)} fusion(bf16[4096,8,384]{2,1,0:T(8,128)(2,1)} %bitcast.64, bf16[256,4096]{1,0:T(8,128)(2,1)} %x_ref.1, f32[4096]{0:T(1024)S(1)} %bitcast.63, f32[256]{0:T(256)S(1)} %add_rsqrt_fusion), kind=kOutput, calls=%fused_computation.11 | convolution fusion | flops 6447431680 | bytes 28853248 | tf_op jit(solution)/shard_map/sd,dhe->she/dot_general | solution.py:633
  21.5 9.5 %front.1 = (bf16[256,1024]{1,0:T(8,128)(2,1)}, bf16[4,256,256]{2,1,0:T(8,128)(2,1)}, bf16[4,256,256]{2,1,0:T(8,128)(2,1)}, bf16[8,2048,128]{2,1,0:T(8,128)(2,1)}, bf16[8,2048,128]{2,1,0:T(8,128)(2,1)}) custom-call(s32[1]{0:T(128)S(6)} %copy.41.s_len, bf16[8,256,384]{2,1,0:T(8,128)(2,1)} %fusion.14.qkv_a, f32[256,128]{1,0:T(8,128)} %constant.11.clone.cos_a.cos_tab, ...), custom_call_target="tpu_custom_call" | custom-call | flops 536870912 | bytes 16777216 | tf_op jit(solution)/shard_map/front/pallas_call | solution.py:641
  31.1 213.2 %block.1 = (bf16[256,4096]{1,0:T(8,128)(2,1)}, bf16[8,4096]{1,0:T(8,128)(2,1)}, bf16[256,1024]{1,0:T(8,128)(2,1)}, bf16[256,1024]{1,0:T(8,128)(2,1)}, f32[2,64,128]{2,1,0:T(8,128)}) custom-call(s32[8]{0:T(128)} %c_len.3, bf16[256,4096]{1,0:T(8,128)(2,1)} %x_ref.1, bf16[8,4096]{1,0:T(8,128)(2,1)} %y_ref.1, bf16[256,1024]{1,0:T(8,128)(2,1)} %get-tuple-element.20.attn_a_ref, ...), custom_call_target="tpu_custom_call" | custom-call | flops 10034872320 | bytes 228065280 | tf_op jit(solution)/shard_map/block/pallas_call | solution.py:478
  244.3 0.0 copy-start.1
  244.3 0.0 copy-start
  244.3 4.2 %insert.1 = (bf16[8,2048,128]{2,1,0:T(8,128)(2,1)}, bf16[8,2048,128]{2,1,0:T(8,128)(2,1)}, bf16[256,4096]{1,0:T(8,128)(2,1)}, bf16[8,4096]{1,0:T(8,128)(2,1)}) custom-call(s32[8]{0:T(128)} %c_len.3, f32[2,64,128]{2,1,0:T(8,128)} %get-tuple-element.23.fresh, bf16[8,4096]{1,0:T(8,128)(2,1)} %get-tuple-element.24.y_in, ...), custom_call_target="tpu_custom_call", output_to_operand_aliasing={{0}: (4, {}), {1}: (5, {})} | custom-call | tf_op jit(solution)/shard_map/insert/pallas_call | solution.py:607
  248.5 0.0 copy-done.1
  248.5 0.9 copy.31
  249.4 0.0 copy-done
  249.4 0.9 copy.32
  (1 shorter events, 0.0 us)
Async XLA Ops:
  244.3 4.2 %copy-start.1 = (bf16[256,1024]{1,0:T(8,128)(2,1)S(1)}, bf16[256,1024]{1,0:T(8,128)(2,1)}, u32[]{:S(2)}) copy-start(bf16[256,1024]{1,0:T(8,128)(2,1)} %get-tuple-element.30) | copy-start | bytes 1572868
  244.3 5.1 %copy-start = (bf16[256,1024]{1,0:T(8,128)(2,1)S(1)}, bf16[256,1024]{1,0:T(8,128)(2,1)}, u32[]{:S(2)}) copy-start(bf16[256,1024]{1,0:T(8,128)(2,1)} %get-tuple-element.31) | copy-start | bytes 1572868
